TPU v7x, 16 devices: a 4x2x1 block of a 4x4x8 slice. The times are simulated.
16 devices in a mesh: dp: 2 (over y, z), ep: 8 (over x, core).
Axes of the slice: x: 4, y: 2, z: 1, core: 2. Of those that a mesh axis runs over, the one named last changes fastest.
The devices are a block of a 4x4x8 slice.
Arguments:
- tokens: bfloat16 [2048, 2048], P(('dp', 'ep')), parts along dimension 0
- expert_ids: int32 [2048, 8], P(('dp', 'ep')), parts along dimension 0
- norm_gain: bfloat16 [2048], replicated
- w_router: bfloat16 [2048, 64], replicated
- w_gate: bfloat16 [64, 2048, 1024], P('ep')
- w_up: bfloat16 [64, 2048, 1024], P('ep')
- w_down: bfloat16 [64, 1024, 2048], P('ep')
Outputs:
- output: bfloat16 [2048, 2048], P(('dp', 'ep')), parts along dimension 0
There are 2 independent parts. A program takes and returns all parts, laid end to end along the dimension named above; an argument that names none is the same for every part.
All inputs are finite; a program needn't handle non-finite values.
Results may differ from a plain program's by a relative error of at most 0.00576213.
Values are sent between devices in bfloat16 or wider.
A program may use at most 768 MiB of HBM per device.

v0:
```python
import jax
import jax.numpy as jnp
from jax import lax
from jax.sharding import PartitionSpec as P

NORM_EPS = 1e-5


def rms_norm(tok_rows, norm_gain):
    tok32 = tok_rows.astype(jnp.float32)
    inv_rms = lax.rsqrt(jnp.mean(tok32 * tok32, axis=1, keepdims=True) + NORM_EPS)
    return (tok32 * inv_rms * norm_gain.astype(jnp.float32)).astype(jnp.bfloat16)


def expert_ffn(rows, w_gate, w_up, w_down, group_sizes):
    hidden_gate = lax.ragged_dot(rows, w_gate, group_sizes, preferred_element_type=jnp.float32)
    hidden_up = lax.ragged_dot(rows, w_up, group_sizes, preferred_element_type=jnp.float32)
    swiglu_out = (jax.nn.silu(hidden_gate) * hidden_up).astype(jnp.bfloat16)
    return lax.ragged_dot(swiglu_out, w_down, group_sizes, preferred_element_type=jnp.float32).astype(jnp.bfloat16)


def route_plan(expert_ids, ep_size, e_local, send_max):
    tok_count, top_k = expert_ids.shape
    pairs = tok_count * top_k
    flat_ids = expert_ids.reshape(pairs)
    sort_order = jnp.argsort(flat_ids, stable=True)
    sorted_dev = flat_ids[sort_order] // e_local
    expert_count = jnp.bincount(flat_ids, length=ep_size * e_local).astype(jnp.int32)
    dev_count = expert_count.reshape(ep_size, e_local).sum(axis=1)
    dev_start = jnp.cumsum(dev_count) - dev_count
    slot_sorted = sorted_dev * send_max + jnp.arange(pairs) - dev_start[sorted_dev]
    slot_of_pair = jnp.zeros((pairs,), jnp.int32).at[sort_order].set(slot_sorted)
    sorted_pos = jnp.minimum(dev_start[:, None] + jnp.arange(send_max)[None, :], pairs - 1)
    send_tok = (sort_order[sorted_pos] // top_k).reshape(ep_size * send_max)
    return expert_count.reshape(ep_size, e_local), slot_of_pair, send_tok


def recv_plan(recv_count, send_max, recv_max):
    ep_size, e_local = recv_count.shape
    row_end = jnp.cumsum(recv_count, axis=1)
    row_begin = row_end - recv_count
    slot_rank = jnp.arange(send_max)
    slot_expert = jnp.sum(row_end[:, None, :] <= slot_rank[None, :, None], axis=2)
    expert_safe = jnp.minimum(slot_expert, e_local - 1)
    expert_total = recv_count.sum(axis=0)
    expert_start = jnp.cumsum(expert_total) - expert_total
    src_before = jnp.cumsum(recv_count, axis=0) - recv_count
    offset = expert_start[None, :] + src_before - row_begin
    compact_pos = jnp.where(slot_expert < e_local, jnp.take_along_axis(offset, expert_safe, axis=1) + slot_rank[None, :], recv_max).reshape(ep_size * send_max)
    compact_src = jnp.zeros((recv_max,), jnp.int32).at[compact_pos].set(jnp.arange(ep_size * send_max), mode='drop')
    return expert_total, compact_src, jnp.minimum(compact_pos, recv_max - 1)


def solution(mesh):
    ep_size = mesh.shape['ep']

    def device_step(tokens, expert_ids, norm_gain, w_router, w_gate, w_up, w_down):
        tok_count, top_k = expert_ids.shape
        width = tokens.shape[1]
        e_local = w_gate.shape[0]
        pairs = tok_count * top_k
        send_max = 2 * pairs // ep_size
        recv_max = 3 * pairs // 2
        normed = rms_norm(tokens, norm_gain)
        router_prob = jax.nn.softmax(jnp.dot(normed, w_router, preferred_element_type=jnp.float32), axis=1)
        gate_vals = jnp.take_along_axis(router_prob, expert_ids, axis=1)
        send_count, slot_of_pair, send_tok = route_plan(expert_ids, ep_size, e_local, send_max)
        send_rows = normed[send_tok].reshape(ep_size, send_max, width)
        recv_count = lax.all_to_all(send_count, 'ep', 0, 0, tiled=True)
        recv_rows = lax.all_to_all(send_rows, 'ep', 0, 0, tiled=True)
        expert_total, compact_src, back_pos = recv_plan(recv_count, send_max, recv_max)
        compact_rows = recv_rows.reshape(ep_size * send_max, width)[compact_src]
        expert_out = expert_ffn(compact_rows, w_gate, w_up, w_down, expert_total)
        back_rows = expert_out[back_pos].reshape(ep_size, send_max, width)
        home_rows = lax.all_to_all(back_rows, 'ep', 0, 0, tiled=True)
        pair_out = home_rows.reshape(ep_size * send_max, width)[slot_of_pair].reshape(tok_count, top_k, width)
        moe_sum = jnp.sum(gate_vals[:, :, None] * pair_out, axis=1)
        return (tokens.astype(jnp.float32) + moe_sum).astype(jnp.bfloat16)

    row_spec = P(('dp', 'ep'), None)
    expert_spec = P('ep', None, None)
    return jax.shard_map(device_step, mesh=mesh, in_specs=(row_spec, row_spec, P(None), P(None, None), expert_spec, expert_spec, expert_spec), out_specs=row_spec, check_vma=False)
```

profile of v0, /device:TPU:112, one launch (start us, length us, event | category | flops | bytes accessed | tf_op | source)
XLA Modules:
  0.0 399.0 jit_solution(10612646479891758264)
XLA Ops:
  0.0 0.8 broadcast_maximum_fusion
  1.0 7.6 %scatter_custom_fusion = s32[64]{0:T(128)S(1)} fusion(s32[1024]{0:T(1024)S(1)} %reshape.509, s32[1024]{0:T(1024)S(1)} %broadcast.445, s32[]{:T(128)} %constant.46.clone.1), kind=kCustom, calls=%fused_computation.90 | custom fusion | flops 1024 | bytes 260 | tf_op jit(solution)/shard_map/scatter-add | solution.py:28
  9.3 5.3 %all-to-all-start.1 = ((s32[8,1,8]{2,1,0:T(1,128)}), s32[8,1,8]{2,1,0:T(1,128)S(1)}, u32[]{:S(2)}, u32[]{:S(2)}) async-start(s32[8,1,8]{2,1,0:T(1,128)} %bitcast.1), calls=%async_computation.1 | async-start | bytes 8192 | tf_op jit(solution)/shard_map/all_to_all | solution.py:69
  14.6 0.8 copy.37
  15.4 1.2 fusion.1
  16.7 0.7 convert_element_type.29
  17.9 4.4 %sort.17 = (s32[1024]{0:T(1024)}, s32[1024]{0:T(1024)S(1)}) sort(s32[1024]{0:T(1024)S(1)} %reshape.421, s32[1024]{0:T(1024)S(1)} %iota.21), dimensions={0}, to_apply=%region_3.0 | sort | flops 10240 | bytes 16384 | tf_op jit(solution)/shard_map/jit(argsort)/sort | solution.py:26
  22.2 8.6 %gather_fusion = s32[2048]{0:T(1024)S(1)} fusion(s32[1024]{0:T(1024)S(1)} %get-tuple-element.6, s32[2048]{0:T(1024)S(1)} %broadcast_clamp_fusion.2), kind=kCustom, calls=%fused_computation | custom fusion | bytes 24576 | tf_op jit(solution)/shard_map/gather | solution.py:34
  31.1 11.0 %gather_fusion.1 = bf16[2048,2048]{1,0:T(8,128)(2,1)} fusion(bf16[128,2048]{1,0:T(8,128)(2,1)S(1)} %fusion.3, s32[2048]{0:T(1024)S(1)} %broadcast_clamp_fusion.1), kind=kCustom, calls=%fused_computation.1 | custom fusion | bytes 16785408 | tf_op jit(solution)/shard_map/gather | solution.py:68
  42.1 5.1 %all-to-all-start = ((bf16[8,256,2048]{2,1,0:T(8,128)(2,1)}), bf16[8,256,2048]{2,1,0:T(8,128)(2,1)}, u32[]{:S(2)}, u32[]{:S(2)}) async-start(bf16[8,256,2048]{2,1,0:T(8,128)(2,1)} %bitcast.65), calls=%async_computation | async-start | bytes 16777216 | tf_op jit(solution)/shard_map/all_to_all | solution.py:70
  48.0 1.5 ragged-dot-metadata
  49.6 0.8 reduce-window.16
  51.3 9.1 %gather_fusion.7 = s32[2048]{0:T(1024)S(1)} fusion(s32[8,8]{1,0:T(8,128)S(1)} %subtract_subtract_fusion, s32[2048]{0:T(1024)S(1)} %bitcast.63), kind=kCustom, calls=%fused_computation.7 | custom fusion | bytes 32768 | tf_op jit(solution)/shard_map/jit(take_along_axis)/gather | solution.py:49
  60.5 8.0 %scatter_custom_fusion.1 = s32[1536]{0:T(1024)S(1)} fusion(s32[2048]{0:T(1024)S(1)} %bitcast.79, s32[2048]{0:T(1024)S(1)} %iota.22, s32[]{:T(128)} %constant.46.clone.1), kind=kCustom, calls=%fused_computation.79 | custom fusion | bytes 6148 | tf_op jit(solution)/shard_map/scatter | solution.py:50
  68.6 73.1 %all-to-all-done = bf16[8,256,2048]{2,1,0:T(8,128)(2,1)} async-done(((bf16[8,256,2048]{2,1,0:T(8,128)(2,1)}), bf16[8,256,2048]{2,1,0:T(8,128)(2,1)}, u32[]{:S(2)}, u32[]{:S(2)}) %all-to-all-start) | async-done | bytes 8388640 | tf_op jit(solution)/shard_map/all_to_all | solution.py:70
  141.7 17.1 %gather_fusion.2 = bf16[1536,2048]{1,0:T(8,128)(2,1)} fusion(bf16[2048,2048]{1,0:T(8,128)(2,1)} %bitcast.7, s32[2048]{0:T(1024)S(1)} %pad_clamp_fusion), kind=kCustom, calls=%fused_computation.2 | custom fusion | bytes 12589056 | tf_op jit(solution)/shard_map/gather | solution.py:72
  158.8 24.7 %ragged-dot-none.2 = f32[1536,1024]{1,0:T(8,128)} custom-call(s32[1]{0:T(128)} %get-tuple-element.7, s32[9]{0:T(128)} %get-tuple-element.8, s32[13]{0:T(128)} %get-tuple-element.9, s32[13]{0:T(128)} %get-tuple-element.10, s32[1]{0:T(128)} %get-tuple-element.7, bf16[1536,2048]{1,0:T(8,128)(2,1)} %gather_fusion.2, bf16[8,2048,1024]{2,1,0:T(8,128)(2,1)} %param.11), custom_call_target="tpu_custom_call" | custom-call | flops 6442450944 | bytes 46137376 | tf_op jit(solution)/shard_map/ragged_dot_general/ragged-dot-none
  183.6 24.7 %ragged-dot-none.1 = f32[1536,1024]{1,0:T(8,128)} custom-call(s32[1]{0:T(128)} %get-tuple-element.7, s32[9]{0:T(128)} %get-tuple-element.8, s32[13]{0:T(128)} %get-tuple-element.9, s32[13]{0:T(128)} %get-tuple-element.10, s32[1]{0:T(128)} %get-tuple-element.7, bf16[1536,2048]{1,0:T(8,128)(2,1)} %gather_fusion.2, bf16[8,2048,1024]{2,1,0:T(8,128)(2,1)} %param.12), custom_call_target="tpu_custom_call" | custom-call | flops 6442450944 | bytes 46137376 | tf_op jit(solution)/shard_map/ragged_dot_general/ragged-dot-none
  208.3 6.8 %multiply_convert_fusion = bf16[1536,1024]{1,0:T(8,128)(2,1)} fusion(f32[1536,1024]{1,0:T(8,128)} %ragged-dot-none.1, f32[1536,1024]{1,0:T(8,128)} %ragged-dot-none.2), kind=kLoop, calls=%fused_computation.13 | loop fusion | flops 9437184 | bytes 15728640 | tf_op jit(solution)/shard_map/convert_element_type | solution.py:18
  215.1 26.1 %ragged-dot-none = f32[1536,2048]{1,0:T(8,128)} custom-call(s32[1]{0:T(128)} %get-tuple-element.7, s32[9]{0:T(128)} %get-tuple-element.8, s32[13]{0:T(128)} %get-tuple-element.9, s32[13]{0:T(128)} %get-tuple-element.10, s32[1]{0:T(128)} %get-tuple-element.7, bf16[1536,1024]{1,0:T(8,128)(2,1)} %multiply_convert_fusion, bf16[8,1024,2048]{2,1,0:T(8,128)(2,1)} %param.13), custom_call_target="tpu_custom_call" | custom-call | flops 6442450944 | bytes 49283104 | tf_op jit(solution)/shard_map/ragged_dot_general/ragged-dot-none
  241.1 8.2 %convert_element_type.33 = bf16[1536,2048]{1,0:T(8,128)(2,1)} convert(f32[1536,2048]{1,0:T(8,128)} %ragged-dot-none) | non-fusion elementwise | flops 3145728 | bytes 18874368 | tf_op jit(solution)/shard_map/convert_element_type | solution.py:19
  249.4 19.9 %gather_fusion.3 = bf16[2048,2048]{1,0:T(8,128)(2,1)} fusion(bf16[1536,2048]{1,0:T(8,128)(2,1)} %convert_element_type.33, s32[2048]{0:T(1024)S(1)} %broadcast_clamp_fusion), kind=kCustom, calls=%fused_computation.3 | custom fusion | bytes 16785408 | tf_op jit(solution)/shard_map/gather | solution.py:74
  269.3 14.3 %all-to-all-start.2 = ((bf16[8,256,2048]{2,1,0:T(8,128)(2,1)}), bf16[8,256,2048]{2,1,0:T(8,128)(2,1)}, u32[]{:S(2)}, u32[]{:S(2)}) async-start(bf16[8,256,2048]{2,1,0:T(8,128)(2,1)} %bitcast.64), calls=%async_computation.2 | async-start | bytes 16777216 | tf_op jit(solution)/shard_map/all_to_all | solution.py:75
  283.8 4.5 %gather_fusion.4 = s32[1024]{0:T(1024)S(1)} fusion(s32[1024]{0:T(1024)S(1)} %reshape.421, s32[1024]{0:T(1024)S(1)} %get-tuple-element.23), kind=kCustom, calls=%fused_computation.4 | custom fusion | bytes 12288 | tf_op jit(solution)/shard_map/gather | solution.py:27
  288.8 7.0 %gather_fusion.6 = f32[1024]{0:T(1024)S(1)} fusion(f32[128,64]{0,1:T(8,128)S(1)} %fusion.5, s32[1024]{0:T(1024)S(1)} %reshape.495), kind=kCustom, calls=%fused_computation.6 | custom fusion | bytes 16384 | tf_op jit(solution)/shard_map/jit(take_along_axis)/gather | solution.py:66
  296.1 0.7 fusion.27
  296.8 4.4 %compare_select_fusion.11 = (s32[1024,1]{0,1:T(1,128)S(1)}, s32[1024,1]{0,1:T(1,128)S(1)}) fusion(s32[]{:T(128)} %bitcast.19, s32[]{:T(128)} %bitcast.20, s32[]{:T(128)} %bitcast.21, s32[]{:T(128)} %bitcast.22, s32[]{:T(128)} %bitcast.23, s32[]{:T(128)} %bitcast.25, s32[]{:T(128)} %bitcast.24, s32[1024,1]{0,1:T(1,128)S(1)} %bitcast.69), kind=kLoop, calls=%fused_computation.40 | loop fusion | flops 30720 | bytes 12316 | tf_op jit(solution)/shard_map/gather | solution.py:31
  301.9 4.5 %scatter_custom_fusion.2 = s32[1024]{0:T(1024)S(1)} fusion(s32[1024]{0:T(1024)S(1)} %get-tuple-element.24, s32[1024]{0:T(1024)S(1)} %fusion.17, s32[]{:T(128)} %constant.46.clone.1), kind=kCustom, calls=%fused_computation.84 | custom fusion | bytes 4100 | tf_op jit(solution)/shard_map/scatter | solution.py:32
  306.4 71.8 %all-to-all-done.2 = bf16[8,256,2048]{2,1,0:T(8,128)(2,1)} async-done(((bf16[8,256,2048]{2,1,0:T(8,128)(2,1)}), bf16[8,256,2048]{2,1,0:T(8,128)(2,1)}, u32[]{:S(2)}, u32[]{:S(2)}) %all-to-all-start.2) | async-done | bytes 8388640 | tf_op jit(solution)/shard_map/all_to_all | solution.py:75
  378.2 13.3 %gather_fusion.5 = bf16[1024,2048]{1,0:T(8,128)(2,1)} fusion(bf16[2048,2048]{1,0:T(8,128)(2,1)} %bitcast.16, s32[1024]{0:T(1024)S(1)} %fusion.18), kind=kCustom, calls=%fused_computation.5 | custom fusion | bytes 8392704 | tf_op jit(solution)/shard_map/gather | solution.py:76
  391.6 6.5 %fusion = f32[128,2048]{1,0:T(8,128)S(1)} fusion(bf16[1024,2048]{1,0:T(8,128)(2,1)} %gather_fusion.5, f32[128,8]{1,0:T(8,128)S(1)} %copy.34), kind=kLoop, calls=%fused_computation.12 | loop fusion | flops 6029312 | bytes 5246976 | tf_op jit(solution)/shard_map/reduce_sum | solution.py:77
  398.1 0.9 fusion.4
  (60 shorter events, 4.8 us)
Async XLA Ops:
  0.0 288.4 %copy-start = (bf16[2048,64]{0,1:T(8,128)(2,1)S(1)}, bf16[2048,64]{0,1:T(8,128)(2,1)}, u32[]{:S(2)}) copy-start(bf16[2048,64]{0,1:T(8,128)(2,1)} %param.10) | copy-start | bytes 786436
  0.0 30.9 %copy-start.1 = (bf16[128,2048]{1,0:T(8,128)(2,1)S(1)}, bf16[128,2048]{1,0:T(8,128)(2,1)}, u32[]{:S(2)}) copy-start(bf16[128,2048]{1,0:T(8,128)(2,1)} %param.7) | copy-start | bytes 1572868
  9.3 32.9 %all-to-all-start.1 = ((s32[8,1,8]{2,1,0:T(1,128)}), s32[8,1,8]{2,1,0:T(1,128)S(1)}, u32[]{:S(2)}, u32[]{:S(2)}) async-start(s32[8,1,8]{2,1,0:T(1,128)} %bitcast.1), calls=%async_computation.1 | async-start | bytes 8192 | tf_op jit(solution)/shard_map/all_to_all | solution.py:69
  42.1 99.5 %all-to-all-start = ((bf16[8,256,2048]{2,1,0:T(8,128)(2,1)}), bf16[8,256,2048]{2,1,0:T(8,128)(2,1)}, u32[]{:S(2)}, u32[]{:S(2)}) async-start(bf16[8,256,2048]{2,1,0:T(8,128)(2,1)} %bitcast.65), calls=%async_computation | async-start | bytes 16777216 | tf_op jit(solution)/shard_map/all_to_all | solution.py:70
  269.3 14.3 %copy-start.3 = (s32[128,8]{0,1:T(8,128)S(1)}, s32[128,8]{0,1:T(8,128)}, u32[]{:S(2)}) copy-start(s32[128,8]{0,1:T(8,128)} %param.8) | copy-start | bytes 12292
  269.3 108.9 %all-to-all-start.2 = ((bf16[8,256,2048]{2,1,0:T(8,128)(2,1)}), bf16[8,256,2048]{2,1,0:T(8,128)(2,1)}, u32[]{:S(2)}, u32[]{:S(2)}) async-start(bf16[8,256,2048]{2,1,0:T(8,128)(2,1)} %bitcast.64), calls=%async_computation.2 | async-start | bytes 16777216 | tf_op jit(solution)/shard_map/all_to_all | solution.py:75
  378.2 19.9 %copy-start.2 = (bf16[128,2048]{1,0:T(8,128)(2,1)S(1)}, bf16[128,2048]{1,0:T(8,128)(2,1)}, u32[]{:S(2)}) copy-start(bf16[128,2048]{1,0:T(8,128)(2,1)} %param.7) | copy-start | bytes 1572868
where the time goes:
time: 400 us; the launch traced here: 399 us
  waiting for transfers between devices  145 us (36%)
  local copies, waits for them, and re-layouts  106 us (26%)
  Pallas kernels  77 us (19%)
  other arithmetic  45.4 us (11%)
  starting transfers between devices  24.8 us (6%)
    another operation x3, Pallas kernels  75.5 us
    all_to_all x1, waiting for transfers between devices, device_step(): recv_rows = lax.all_to_all(send_rows, 'ep', 0, 0, tiled=True)  73.1 us
    all_to_all x1, waiting for transfers between devices, device_step(): home_rows = lax.all_to_all(back_rows, 'ep', 0, 0, tiled=True)  71.8 us
    gather x1, local copies, waits for them, and re-layouts, device_step(): back_rows = expert_out[back_pos].reshape(ep_size, send_max, width)  19.9 us
    gather x1, local copies, waits for them, and re-layouts, device_step(): compact_rows = recv_rows.reshape(ep_size * send_max, width)[compact_src]  17.1 us
    all_to_all x1, starting transfers between devices, device_step(): home_rows = lax.all_to_all(back_rows, 'ep', 0, 0, tiled=True)  14.3 us
    gather x1, local copies, waits for them, and re-layouts, device_step(): home_rows.reshape(ep_size * send_max, width)[slot_of_pair]  13.3 us
    gather x1, local copies, waits for them, and re-layouts, device_step(): send_rows = normed[send_tok].reshape(ep_size, send_max, width)  11 us
  transfers between devices with their start and end apart: 3, of which 2 were waited for; matrix products, arithmetic and copies ran while one was open for 18% of the time, Pallas kernels for 0%

commit v1 on v0

v1 whole, which is shorter than its diff:
```python
import functools

import jax
import jax.numpy as jnp
from jax import lax
from jax.experimental import pallas as pl
from jax.experimental.pallas import tpu as pltpu
from jax.sharding import PartitionSpec as P

NORM_EPS = 1e-5
TILE = 128
SUB = 8
LANE = 128
F32 = jnp.float32
BF16 = jnp.bfloat16
MESH = pl.DeviceIdType.MESH


def dot(a, b, dims=(((1,), (0,)), ((), ()))):
    return lax.dot_general(a, b, dims, preferred_element_type=F32)


NT_DIMS = (((1,), (1,)), ((), ()))


class Place:
    def __init__(self, ep):
        self.ep = ep
        self.me = lax.axis_index("ep")
        self.xi, self.core = self.me // 2, self.me % 2
        self.chips = ep // 2
        self.right, self.left, self.far = self.dev(1, self.core), self.dev(-1, self.core), self.dev(2, self.core)
        self.partner = self.dev(0, 1 - self.core)

    def dev(self, dx, c):
        return lax.rem(self.xi + dx + self.chips, self.chips) * 2 + c

    def signal_all(self):
        barrier = pltpu.get_barrier_semaphore()
        for d in range(1, self.ep):
            pl.semaphore_signal(barrier, inc=1, device_id={"ep": lax.rem(self.me + d, self.ep)}, device_id_type=MESH)
        return barrier


class Gather:
    def __init__(self, pc, ref, send, recv, tok, own=None):
        self.pc, self.ref, self.send, self.recv, self.tok, self.own = pc, ref, send, recv, tok, own

    def copy(self, j, block, r, target, own=False):
        hr = self.tok // 2
        rows = pl.ds(pl.multiple_of(block * self.tok + r * hr, hr), hr)
        dst = self.ref.at[rows, :]
        src = self.own.at[pl.ds(r * hr, hr), :] if own and self.own is not None else dst
        return pltpu.make_async_remote_copy(
            src, dst, self.send.at[j], self.recv.at[j], device_id={"ep": target}, device_id_type=MESH)

    def start(self):
        p = self.pc
        self.copy(0, p.me, 0, p.right, True).start()
        self.copy(2, p.me, 1, p.left, True).start()
        self.copy(1, p.me, 1, p.right, True).start()
        self.copy(3, p.me, 0, p.left, True).start()
        self.copy(6, p.me, 0, p.partner, True).start()
        self.copy(7, p.me, 1, p.partner, True).start()

    def forward(self):
        p = self.pc
        self.copy(0, p.left, 0, p.right).wait_recv()
        self.copy(4, p.left, 0, p.right).start()
        self.copy(8, p.left, 0, p.partner).start()
        self.copy(2, p.right, 1, p.left).wait_recv()
        self.copy(5, p.right, 1, p.left).start()
        self.copy(11, p.right, 1, p.partner).start()

    def rest(self):
        p = self.pc
        self.copy(1, p.left, 1, p.right).wait_recv()
        self.copy(9, p.left, 1, p.partner).start()
        self.copy(3, p.right, 0, p.left).wait_recv()
        self.copy(10, p.right, 0, p.partner).start()

    def last(self):
        p = self.pc
        self.copy(4, p.far, 0, p.right).wait_recv()
        self.copy(12, p.far, 0, p.partner).start()
        self.copy(5, p.far, 1, p.left).wait_recv()
        self.copy(13, p.far, 1, p.partner).start()

    def finish(self):
        p = self.pc
        for j, (dx, r) in enumerate(((0, 0), (0, 1), (-1, 0), (-1, 1), (1, 0), (1, 1), (2, 0), (2, 1))):
            self.copy(6 + j, p.dev(dx, 1 - p.core), r, p.partner).wait_recv()

    def drain(self):
        for j in range(14):
            self.copy(j, self.pc.me, 0, self.pc.right).wait_send()


def plan_kernel(
    ep, tiles,
    x_ref, ids_ref, gain_ref, wr_ref,
    u0_ref, u1_ref, slot_ref, src_v, first_v, last_v, te_v, gate_v,
    p_ref, id_land, p_land,
    small_send, small_recv, ag_send, ag_recv,
):
    pc = Place(ep)
    me = pc.me
    tok, width = x_ref.shape
    half_w = width // 2
    e_local = slot_ref.shape[0]
    q_max = src_v.shape[1]
    barrier = pc.signal_all()

    x32 = x_ref[...].astype(F32)
    inv = lax.rsqrt(jnp.mean(x32 * x32, axis=1, keepdims=True) + NORM_EPS)
    u_own = (x32 * inv * gain_ref[...].astype(F32)).astype(BF16)
    own_rows = pl.ds(pl.multiple_of(me * tok, tok), tok)
    u0_ref[own_rows, :] = u_own[:, :half_w]
    u1_ref[...] = u_own[:, half_w:]

    pl.semaphore_wait(barrier, ep - 1)

    ag = Gather(pc, u0_ref, ag_send, ag_recv, tok)
    ag.start()

    logits = dot(u_own, wr_ref[...])
    n_exp = logits.shape[1]
    logits = jnp.concatenate([logits, jnp.zeros((tok, LANE - n_exp), F32)], axis=1).T[:n_exp]
    ex = jnp.exp(logits - jnp.max(logits, axis=0, keepdims=True))
    p_ref[...] = ex / jnp.sum(ex, axis=0, keepdims=True)
    id_land[me] = ids_ref[...]
    p_land[me] = p_ref[pl.ds(pl.multiple_of(me * e_local, e_local), e_local), :]

    def small(d, kind, target):
        if kind == 0:
            src, dst = ids_ref, id_land.at[me]
        else:
            src, dst = p_ref.at[pl.ds(pl.multiple_of(target * e_local, e_local), e_local), :], p_land.at[me]
        return pltpu.make_async_remote_copy(
            src, dst, small_send.at[kind, d], small_recv.at[kind, d], device_id={"ep": target}, device_id_type=MESH)

    for kind in range(2):
        for d in range(1, ep):
            small(d, kind, lax.rem(me + d, ep)).start()
    for kind in range(2):
        for d in range(1, ep):
            small(d, kind, lax.rem(me + d, ep)).wait_recv()

    base = me * e_local
    sub_i = lax.broadcasted_iota(jnp.int32, (e_local, LANE), 0)
    lane_i = lax.broadcasted_iota(jnp.int32, (e_local, LANE), 1)
    tri = (lax.broadcasted_iota(jnp.int32, (LANE, LANE), 0) < lax.broadcasted_iota(jnp.int32, (LANE, LANE), 1)).astype(BF16)
    member = []
    for b in range(ep):
        ids_b = id_land[b]
        m = jnp.zeros((e_local, LANE), F32)
        for k in range(ids_b.shape[0]):
            m = m + jnp.where(ids_b[k:k + 1, :] == base + sub_i, 1.0, 0.0)
        member.append(m)
    stack = jnp.concatenate(member, axis=0)
    before = dot(stack.astype(BF16), tri)
    total = jnp.sum(stack, axis=1, keepdims=True)
    run = jnp.zeros((e_local, 1), F32)
    pos = []
    for b in range(ep):
        pos.append(before[b * e_local:(b + 1) * e_local] + run)
        run = run + total[b * e_local:(b + 1) * e_local]
    tiles_e = jnp.floor((run + (TILE - 1)) * (1.0 / TILE))
    start = jnp.zeros((e_local, 1), F32)
    sub_c = lax.broadcasted_iota(jnp.int32, (e_local, 1), 0)
    for e in range(e_local):
        start = start + jnp.where(sub_c > e, tiles_e[e:e + 1, :], 0.0)
    tile_end = start + tiles_e
    te = jnp.sum(jnp.where(tile_end <= lane_i.astype(F32), 1.0, 0.0), axis=0, keepdims=True)
    te_v[...] = jnp.clip(te.astype(jnp.int32), 0, e_local - 1)
    count = jnp.concatenate([jnp.sum(m, axis=0, keepdims=True) for m in member], axis=0)
    first_rank = dot(count.astype(BF16), tri)
    last_row = jnp.where(count > 0, first_rank + count - 1.0, q_max * 1.0)
    last_v[...] = jnp.clip(last_row.astype(jnp.int32), 0, q_max)
    q_row = lax.broadcasted_iota(jnp.int32, (q_max, LANE), 0).astype(F32)
    q_lane = lax.broadcasted_iota(jnp.int32, (e_local, q_max), 1).astype(F32)
    for b in range(ep):
        m = member[b]
        slot = jnp.where(m > 0, start * TILE + pos[b], -1.0)
        slot_ref[:, :, b * LANE:(b + 1) * LANE] = jnp.broadcast_to(slot[:, None, :], (e_local, SUB, LANE))
        pre = jnp.zeros((e_local, LANE), F32)
        for e in range(e_local):
            pre = pre + jnp.where(sub_i > e, m[e:e + 1, :], 0.0)
        fr, ct = first_rank[b:b + 1], count[b:b + 1]
        rank = jnp.where(m > 0, fr + pre, 300.0)
        hi = jnp.floor(slot * (1.0 / 64))
        pb = p_land[b]
        g1 = pb.astype(BF16).astype(F32)
        g2 = (pb - g1).astype(BF16).astype(F32)
        g3 = pb - g1 - g2
        feats = jnp.concatenate([rank, hi, slot - hi * 64.0, jnp.broadcast_to(fr, m.shape), g1, g2, g3, pre], axis=0)
        hot = jnp.where((q_row >= fr) & (q_row < fr + ct), 1.0, 0.0).astype(BF16)
        got = dot(feats.astype(BF16), hot, NT_DIMS)
        e8 = e_local
        sel = got[0:e8] == q_lane
        src = jnp.sum(jnp.where(sel, got[e8:2 * e8] * 64.0 + got[2 * e8:3 * e8], 0.0), axis=0, keepdims=True)
        gate = jnp.sum(jnp.where(sel, got[4 * e8:5 * e8] + got[5 * e8:6 * e8] + got[6 * e8:7 * e8], 0.0), axis=0, keepdims=True)
        src_v[b:b + 1, :] = jnp.clip(src.astype(jnp.int32), 0, tiles * TILE - 1)
        first_v[b:b + 1, :] = (got[3 * e8:3 * e8 + 1] == q_lane[0:1]).astype(jnp.int32)
        gate_v[b:b + 1, :] = gate

    ag.forward()
    ag.rest()
    ag.last()
    ag.finish()
    ag.drain()
    for kind in range(2):
        for d in range(1, ep):
            small(d, kind, lax.rem(me + d, ep)).wait_send()


def moe_kernel(
    ep, tiles,
    te_s, src_s, first_s, last_s, gate_s,
    u0_hbm, u1_ref, slot_ref, x_hbm, w1_hbm, w3_hbm, w2_hbm,
    out_ref,
    u_all, x_v, h_ref, ring0, ring1, ring2, ring3,
    recv_a, recv_h, recv_d,
    in_sem, ring_sem, ag_send, ag_recv,
    a_send, a_recv, h_send, h_recv, d_send, d_recv,
):
    pc = Place(ep)
    me, core, chips, dev = pc.me, pc.core, pc.chips, pc.dev
    right, left, partner, far = pc.right, pc.left, pc.partner, pc.far
    ring = (ring0, ring1, ring2, ring3)
    tok, width = x_v.shape
    q_max = src_s.shape[1]
    half_w = width // 2
    ff = h_ref.shape[1]
    e_local, _, fcol = ring0.shape
    n_fs = ff // fcol
    rows_blk = tok * SUB

    def w13_copy(m, buf):
        kk, ffi = m // (2 * n_fs), (m % (2 * n_fs)) // 2
        rows = pl.ds(pl.multiple_of(kk * half_w, half_w), half_w)
        cols = pl.ds(pl.multiple_of(ffi * fcol, fcol), fcol)
        return [pltpu.make_async_copy(w.at[:, rows, cols], ring[buf], ring_sem.at[buf]) for w in (w1_hbm, w3_hbm)]

    def w2_copy(cs, buf):
        cols = pl.ds(pl.multiple_of(cs * fcol, fcol), fcol)
        return pltpu.make_async_copy(w2_hbm.at[:, :, cols], ring[buf], ring_sem.at[buf])

    for m in range(4):
        w13_copy(m, m)[m % 2].start()

    barrier = pc.signal_all()

    pltpu.make_async_copy(u0_hbm, u_all.at[0], in_sem.at[0]).start()
    pltpu.make_async_copy(x_hbm, x_v, in_sem.at[1]).start()
    own_rows = pl.ds(pl.multiple_of(me * tok, tok), tok)
    pl.semaphore_wait(barrier, ep - 1)
    ag = Gather(pc, u_all.at[1], ag_send, ag_recv, tok, own=u1_ref)
    ag.start()
    u_all[1, own_rows, :] = u1_ref[...]
    pltpu.make_async_copy(u0_hbm, u_all.at[0], in_sem.at[0]).wait()

    def tile_expert(i):
        return te_s[0, i]

    def phase_one(ug, acc):
        t_iota = lax.broadcasted_iota(jnp.int32, (TILE, ep * tok), 0).astype(F32)

        def gather(k, lo, hi, un):
            def body(g, carry):
                for j in range(un):
                    i = lo + g * un + j
                    row = slot_ref[tile_expert(i)][0:1] - lax.convert_element_type(i * TILE, F32)
                    hot = jnp.where(row == t_iota, 1.0, 0.0).astype(BF16)
                    ug[pl.ds(pl.multiple_of(i * TILE, TILE), TILE), :] = dot(hot, u_all[k]).astype(BF16)
                return carry

            lax.fori_loop(0, (hi - lo) // un, body, 0)

        def units(k):
            def two_units(fp, carry):
                for b1 in (0, 2):
                    fs = 2 * fp + b1 // 2
                    n = k * 2 * n_fs + 2 * fs
                    for which in range(2):
                        w13_copy(n, b1 + which)[which].wait()
                    for which in range(2):
                        for i in range(tiles):
                            rows = pl.ds(i * TILE, TILE)
                            d = dot(ug[rows, :], ring[b1 + which][tile_expert(i)])
                            if k == 0:
                                acc[which, fs, rows, :] = d
                            elif which == 0:
                                acc[0, fs, rows, :] = acc[0, fs, rows, :] + d
                            else:
                                g = acc[0, fs, rows, :]
                                hcols = pl.ds(pl.multiple_of(fs * fcol, fcol), fcol)
                                h_ref[rows, hcols] = (g / (1.0 + jnp.exp(-g)) * (acc[1, fs, rows, :] + d)).astype(BF16)
                        if k == 0:
                            w13_copy(n + 4 + which, b1 + which)[which].start()
                        else:
                            @pl.when(fp == 0)
                            def _():
                                w13_copy(n + 4 + which, b1 + which)[which].start()

                            @pl.when(fp > 0)
                            def _():
                                w2_copy(b1 + which, b1 + which).start()
                return carry

            lax.fori_loop(0, n_fs // 2, two_units, 0)

        mid = tiles // 2
        gather(0, 0, mid, 3)
        ag.forward()
        gather(0, mid, tiles, 5)
        ag.rest()
        units(0)
        ag.last()
        ag.finish()
        gather(1, 0, mid, 3)
        gather(1, mid, tiles, 5)
        units(1)

    pl.run_scoped(
        phase_one,
        pltpu.VMEM((tiles * TILE, half_w), BF16),
        pltpu.VMEM((2, n_fs, tiles * TILE, fcol), F32),
    )

    def phase_two(o3, pbuf, accb):
        n_slice = half_w // fcol
        order = (2, 1, 3, 0)
        o_rows = o3.reshape(o3.shape[0] // SUB, SUB, LANE)
        p_rows = pbuf.reshape(pbuf.shape[0] // SUB, SUB, LANE)
        pbuf[q_max * SUB:(q_max + 1) * SUB, :] = jnp.zeros((SUB, LANE), F32)

        def down(q):
            def body(jp, carry):
                for b1 in range(4):
                    j = jp * 4 + b1
                    w2_copy(q * n_slice + j, b1).wait()
                    for i in range(tiles):
                        o = dot(h_ref[i * TILE:(i + 1) * TILE, :], ring[b1][tile_expert(i)]).astype(BF16).astype(F32)
                        for v in range(fcol // LANE):
                            o3[pl.ds(i * TILE * SUB + j * (fcol // LANE) + v, TILE, stride=SUB), :] = o[:, v * LANE:(v + 1) * LANE]
                    if q == 0:
                        w2_copy(n_slice + j, b1).start()
                return carry

            lax.fori_loop(0, n_slice // 4, body, 0)

        def block(q, s):
            return pl.ds(pl.multiple_of((q * ep + s) * rows_blk, rows_blk), rows_blk)

        def combine(q, s):
            un = 8

            def pairs(i, run):
                for j in range(un):
                    qq = i * un + j
                    row = o_rows[src_s[s, qq]]
                    run = jnp.where(jnp.full((SUB, LANE), first_s[s, qq], jnp.int32) == 1, 0.0, run) + gate_s[s, qq] * row
                    pbuf[pl.ds(pl.multiple_of(qq * SUB, SUB), SUB), :] = run
                return run

            lax.fori_loop(0, q_max // un, pairs, jnp.zeros((SUB, LANE), F32))

            def tokens(i, carry):
                for j in range(un):
                    t = i * un + j
                    dst = pl.ds(pl.multiple_of((q * ep + s) * rows_blk + t * SUB, SUB), SUB)
                    accb[dst, :] = p_rows[last_s[s, t]]
                return carry

            lax.fori_loop(0, tok // un, tokens, 0)

        def a_copy(q, j):
            rows = pl.ds((q * chips + j) * rows_blk, rows_blk)
            return pltpu.make_async_remote_copy(
                accb.at[block(q, dev(order[j], 1 - core)), :], recv_a.at[rows, :], a_send.at[q, j], a_recv.at[q, j],
                device_id={"ep": partner}, device_id_type=MESH)

        def a_add(q, j):
            a_copy(q, j).wait_recv()
            mine = block(q, dev(order[j], core))
            accb[mine, :] = accb[mine, :] + recv_a[(q * chips + j) * rows_blk:(q * chips + j + 1) * rows_blk, :]

        hb = rows_blk // 2

        def half(q, s, r):
            return pl.ds(pl.multiple_of((q * ep + s) * rows_blk + r * hb, hb), hb)

        def h_copy(q, side):
            return pltpu.make_async_remote_copy(
                accb.at[half(q, far, side), :], recv_h.at[pl.ds((q * 2 + side) * hb, hb), :], h_send.at[q, side], h_recv.at[q, side],
                device_id={"ep": left if side else right}, device_id_type=MESH)

        def d_copy(q, side, r):
            s = left if side else right
            return pltpu.make_async_remote_copy(
                accb.at[half(q, s, r), :], recv_d.at[pl.ds((q * 2 + side) * rows_blk + r * hb, hb), :],
                d_send.at[q, side * 2 + r], d_recv.at[q, side * 2 + r], device_id={"ep": s}, device_id_type=MESH)

        def relay(q):
            for side in range(2):
                h_copy(q, side).wait_recv()
                s = left if side else right
                mine = half(q, s, side)
                accb[mine, :] = accb[mine, :] + recv_h[(q * 2 + side) * hb:(q * 2 + side + 1) * hb, :]
                d_copy(q, side, side).start()

        def scatter(q):
            for j in range(chips):
                combine(q, dev(order[j], 1 - core))
                a_copy(q, j).start()
                combine(q, dev(order[j], core))
                a_add(q, j)
                if j == 0:
                    h_copy(q, 0).start()
                    h_copy(q, 1).start()
                elif j == 1:
                    d_copy(q, 0, 1).start()
                elif j == 2:
                    d_copy(q, 1, 0).start()

        def finish(q):
            for side in range(2):
                for r in range(2):
                    d_copy(q, side, r).wait_recv()
            for v in range(half_w // LANE):
                cols = slice(q * half_w + v * LANE, q * half_w + (v + 1) * LANE)
                own = accb[pl.ds((q * ep + me) * rows_blk + v, tok, stride=SUB), :]
                d0 = recv_d[pl.ds(q * 2 * rows_blk + v, tok, stride=SUB), :]
                d1 = recv_d[pl.ds((q * 2 + 1) * rows_blk + v, tok, stride=SUB), :]
                out_ref[:, cols] = (x_v[:, cols].astype(F32) + (own + d0 + d1)).astype(BF16)

        down(0)
        scatter(0)
        down(1)
        relay(0)
        scatter(1)
        relay(1)
        pltpu.make_async_copy(x_hbm, x_v, in_sem.at[1]).wait()
        finish(0)
        finish(1)
        for q in range(2):
            for j in range(chips):
                a_copy(q, j).wait_send()
            for side in range(2):
                h_copy(q, side).wait_send()
                for r in range(2):
                    d_copy(q, side, r).wait_send()

    pl.run_scoped(
        phase_two,
        pltpu.VMEM((tiles * TILE * SUB + SUB, LANE), F32),
        pltpu.VMEM(((q_max + 1) * SUB, LANE), F32),
        pltpu.VMEM((2 * ep * rows_blk + SUB, LANE), F32),
    )

    ag.drain()


def solution(mesh):
    ep = mesh.shape["ep"]

    def device_step(tokens, expert_ids, norm_gain, w_router, w_gate, w_up, w_down):
        tok, top_k = expert_ids.shape
        width = tokens.shape[1]
        e_local, _, ff = w_gate.shape
        pairs = tok * top_k
        send_max = 2 * pairs // ep
        recv_max = 3 * pairs // 2
        tiles = (recv_max + e_local * (TILE - 1)) // TILE
        half_w = width // 2
        fcol = 256
        chips = ep // 2
        rows_blk = tok * SUB
        vm = pl.BlockSpec(memory_space=pltpu.VMEM)
        hbm = pl.BlockSpec(memory_space=pl.ANY)
        sm = pl.BlockSpec(memory_space=pltpu.SMEM)
        dma = pltpu.SemaphoreType.DMA
        i32 = jnp.int32
        groups = (ep, send_max)
        u0, u1, slot, src, first, last, te, gate = pl.pallas_call(
            functools.partial(plan_kernel, ep, tiles),
            out_shape=[
                jax.ShapeDtypeStruct((ep * tok, half_w), BF16),
                jax.ShapeDtypeStruct((tok, half_w), BF16),
                jax.ShapeDtypeStruct((e_local, SUB, ep * tok), F32),
                jax.ShapeDtypeStruct(groups, i32),
                jax.ShapeDtypeStruct(groups, i32),
                jax.ShapeDtypeStruct((ep, tok), i32),
                jax.ShapeDtypeStruct((1, LANE), i32),
                jax.ShapeDtypeStruct(groups, F32),
            ],
            in_specs=[vm] * 4,
            out_specs=[vm] * 8,
            scratch_shapes=[
                pltpu.VMEM((w_router.shape[1], tok), F32),
                pltpu.VMEM((ep, top_k, tok), i32),
                pltpu.VMEM((ep, e_local, tok), F32),
                dma((2, ep)),
                dma((2, ep)),
                dma((14,)),
                dma((14,)),
            ],
            compiler_params=pltpu.CompilerParams(collective_id=0, has_side_effects=True),
            name="moe_plan",
        )(tokens, expert_ids.T, norm_gain[None, :], w_router)
        return pl.pallas_call(
            functools.partial(moe_kernel, ep, tiles),
            out_shape=jax.ShapeDtypeStruct((tok, width), BF16),
            in_specs=[sm] * 5 + [hbm, vm, vm, hbm, hbm, hbm, hbm],
            out_specs=vm,
            scratch_shapes=[
                pltpu.VMEM((2, ep * tok, half_w), BF16),
                pltpu.VMEM((tok, width), BF16),
                pltpu.VMEM((tiles * TILE, ff), BF16),
                *[pltpu.VMEM((e_local, half_w, fcol), BF16)] * 4,
                pltpu.VMEM((2 * chips * rows_blk, LANE), F32),
                pltpu.VMEM((2 * rows_blk, LANE), F32),
                pltpu.VMEM((4 * rows_blk + SUB, LANE), F32),
                dma((2,)),
                dma((4,)),
                dma((14,)),
                dma((14,)),
                dma((2, chips)),
                dma((2, chips)),
                dma((2, 2)),
                dma((2, 2)),
                dma((2, 4)),
                dma((2, 4)),
            ],
            compiler_params=pltpu.CompilerParams(
                collective_id=1, has_side_effects=True, vmem_limit_bytes=67_043_328),
            name="moe_block",
        )(te, src, first, last, gate, u0, u1, slot, tokens, w_gate, w_up, w_down)

    row_spec = P(("dp", "ep"), None)
    expert_spec = P("ep", None, None)
    return jax.shard_map(
        device_step, mesh=mesh,
        in_specs=(row_spec, row_spec, P(None), P(None, None), expert_spec, expert_spec, expert_spec),
        out_specs=row_spec, check_vma=False)
```

time: 400 us -> 129 us (0.32)
  waiting for transfers between devices: 145 us -> 0 us
  local copies, waits for them, and re-layouts: 106 us -> 5.12 us
  Pallas kernels: 77 us -> 124 us
  other arithmetic: 45.4 us -> 0 us
  starting transfers between devices: 24.8 us -> 0 us
    all_to_all x3 -> x0, waiting for transfers between devices: 145 us -> none  [the longest x1 73.1 us: device_step(): recv_rows = lax.all_to_all(send_rows, 'ep', 0, 0, tiled=True)]
    pallas_call x0 -> x2, Pallas kernels: none -> 124 us  [the longest x1 100 us: device_step(): pl.pallas_call(functools.partial(moe_kernel, ep, tiles), out_shape=jax.Sh...]
    gather x13 -> x0, local copies, waits for them, and re-layouts: 91.7 us -> none  [the longest x1 19.9 us: device_step(): back_rows = expert_out[back_pos].reshape(ep_size, send_max, width)]
    another operation x3 -> x0, Pallas kernels: 75.5 us -> none
    all_to_all x3 -> x0, starting transfers between devices: 24.8 us -> none  [the longest x1 14.3 us: device_step(): home_rows = lax.all_to_all(back_rows, 'ep', 0, 0, tiled=True)]
    convert_element_type x5 -> x0, other arithmetic: 16.9 us -> none  [the longest x1 8.22 us: expert_ffn(): lax.ragged_dot(swiglu_out, w_down, group_sizes, preferred_element_type=jn...]
    scatter x2 -> x0, local copies, waits for them, and re-layouts: 12.6 us -> none  [the longest x1 8.05 us: recv_plan(): jnp.zeros((recv_max,), jnp.int32).at[compact_pos]]
    reduce_sum x6 -> x0, other arithmetic: 8.53 us -> none  [the longest x1 6.52 us: device_step(): moe_sum = jnp.sum(gate_vals[:, :, None] * pair_out, axis=1)]
  transfers between devices with their start and end apart: 3 -> 0, of which waited for: 2 -> 0; matrix products, arithmetic and copies ran while one was open for 18% -> 0% of each run, Pallas kernels for 0% -> 0%
where the time goes in v1:
time: 129 us
  Pallas kernels  124 us (96%)
  local copies, waits for them, and re-layouts  5.12 us (4%)
    pallas_call x1, Pallas kernels, device_step(): pl.pallas_call(functools.partial(moe_kernel, ep, tiles), out_shape=jax.Sh...  100 us
    pallas_call x1, Pallas kernels, device_step(): pl.pallas_call(functools.partial(plan_kernel, ep, tiles), out_shape=[jax....  23.4 us
    unnamed x2, local copies, waits for them, and re-layouts  3.83 us

profile of v1, /device:TPU:112, one launch (start us, length us, event | category | flops | bytes accessed | tf_op | source)
XLA Modules:
  0.0 128.7 jit_solution(17734018330580784910)
XLA Ops:
  0.0 1.3 broadcast_in_dim.3.gain_ref
  1.3 2.0 %copy.8.wr_ref = bf16[2048,64]{1,0:T(8,128)(2,1)} copy(bf16[2048,64]{0,1:T(8,128)(2,1)} %param.10) | data formatting | bytes 524288 | tf_op args[3]
  3.2 23.4 %moe_plan.1 = (bf16[1024,1024]{1,0:T(8,128)(2,1)}, bf16[128,1024]{1,0:T(8,128)(2,1)}, f32[8,8,1024]{2,1,0:T(8,128)}, s32[8,256]{1,0:T(8,128)}, s32[8,256]{1,0:T(...) custom-call(bf16[128,2048]{1,0:T(8,128)(2,1)} %x_hbm.1, s32[8,128]{1,0:T(8,128)} %bitcast.1, ...), custom_call_target="tpu_custom_call" | custom-call | tf_op jit(solution)/shard_map/moe_plan/pallas_call | solution.py:486
  26.6 100.2 %moe_block.1 = bf16[128,2048]{1,0:T(8,128)(2,1)} custom-call(s32[1,128]{1,0:T(1,128)} %get-tuple-element.13.te_s, s32[8,256]{1,0:T(8,128)} %get-tuple-element.14.src_s, s32[8,256]{1,0:T(8,128)} %get-tuple-element.15.first_s, s32[8,128]{1,0:T(8,128)} %get-tuple-element.16.last_s, f32[8,256]{1,0:T(8,128)} %get-tuple-element.17.gate_s, ...), custom_call_target="tpu_custom_call" | custom-call | tf_op jit(solution)/shard_map/moe_block/pallas_call | solution.py:512
  126.8 1.9 %copy.10 = bf16[128,2048]{1,0:T(8,128)(2,1)} copy(bf16[128,2048]{1,0:T(8,128)(2,1)} %moe_block.1) | data formatting | bytes 1048576

commit v2 on v1

--- a/solution.py
+++ b/solution.py
@@ -113,7 +113,7 @@
 
     x32 = x_ref[...].astype(F32)
     inv = lax.rsqrt(jnp.mean(x32 * x32, axis=1, keepdims=True) + NORM_EPS)
-    u_own = (x32 * inv * gain_ref[...].astype(F32)).astype(BF16)
+    u_own = (x32 * inv * gain_ref[...].astype(F32)[None, :]).astype(BF16)
     own_rows = pl.ds(pl.multiple_of(me * tok, tok), tok)
     u0_ref[own_rows, :] = u_own[:, :half_w]
     u1_ref[...] = u_own[:, half_w:]
@@ -123,9 +123,7 @@
     ag = Gather(pc, u0_ref, ag_send, ag_recv, tok)
     ag.start()
 
-    logits = dot(u_own, wr_ref[...])
-    n_exp = logits.shape[1]
-    logits = jnp.concatenate([logits, jnp.zeros((tok, LANE - n_exp), F32)], axis=1).T[:n_exp]
+    logits = dot(wr_ref[...], u_own, NT_DIMS)
     ex = jnp.exp(logits - jnp.max(logits, axis=0, keepdims=True))
     p_ref[...] = ex / jnp.sum(ex, axis=0, keepdims=True)
     id_land[me] = ids_ref[...]
@@ -214,27 +212,21 @@
             small(d, kind, lax.rem(me + d, ep)).wait_send()
 
 
-def moe_kernel(
+def up_kernel(
     ep, tiles,
-    te_s, src_s, first_s, last_s, gate_s,
-    u0_hbm, u1_ref, slot_ref, x_hbm, w1_hbm, w3_hbm, w2_hbm,
-    out_ref,
-    u_all, x_v, h_ref, ring0, ring1, ring2, ring3,
-    recv_a, recv_h, recv_d,
+    te_s, u0_hbm, u1_ref, slot_ref, w1_hbm, w3_hbm,
+    h_ref,
+    u_all, ring0, ring1, ring2, ring3,
     in_sem, ring_sem, ag_send, ag_recv,
-    a_send, a_recv, h_send, h_recv, d_send, d_recv,
 ):
     pc = Place(ep)
     me, core, chips, dev = pc.me, pc.core, pc.chips, pc.dev
     right, left, partner, far = pc.right, pc.left, pc.partner, pc.far
     ring = (ring0, ring1, ring2, ring3)
-    tok, width = x_v.shape
-    q_max = src_s.shape[1]
-    half_w = width // 2
+    tok, half_w = u1_ref.shape
     ff = h_ref.shape[1]
     e_local, _, fcol = ring0.shape
     n_fs = ff // fcol
-    rows_blk = tok * SUB
 
     def w13_copy(m, buf):
         kk, ffi = m // (2 * n_fs), (m % (2 * n_fs)) // 2
@@ -242,23 +234,18 @@
         cols = pl.ds(pl.multiple_of(ffi * fcol, fcol), fcol)
         return [pltpu.make_async_copy(w.at[:, rows, cols], ring[buf], ring_sem.at[buf]) for w in (w1_hbm, w3_hbm)]
 
-    def w2_copy(cs, buf):
-        cols = pl.ds(pl.multiple_of(cs * fcol, fcol), fcol)
-        return pltpu.make_async_copy(w2_hbm.at[:, :, cols], ring[buf], ring_sem.at[buf])
-
     for m in range(4):
         w13_copy(m, m)[m % 2].start()
 
     barrier = pc.signal_all()
 
-    pltpu.make_async_copy(u0_hbm, u_all.at[0], in_sem.at[0]).start()
-    pltpu.make_async_copy(x_hbm, x_v, in_sem.at[1]).start()
+    pltpu.make_async_copy(u0_hbm, u_all.at[0], in_sem).start()
     own_rows = pl.ds(pl.multiple_of(me * tok, tok), tok)
     pl.semaphore_wait(barrier, ep - 1)
     ag = Gather(pc, u_all.at[1], ag_send, ag_recv, tok, own=u1_ref)
     ag.start()
     u_all[1, own_rows, :] = u1_ref[...]
-    pltpu.make_async_copy(u0_hbm, u_all.at[0], in_sem.at[0]).wait()
+    pltpu.make_async_copy(u0_hbm, u_all.at[0], in_sem).wait()
 
     def tile_expert(i):
         return te_s[0, i]
@@ -302,10 +289,6 @@
                             @pl.when(fp == 0)
                             def _():
                                 w13_copy(n + 4 + which, b1 + which)[which].start()
-
-                            @pl.when(fp > 0)
-                            def _():
-                                w2_copy(b1 + which, b1 + which).start()
                 return carry
 
             lax.fori_loop(0, n_fs // 2, two_units, 0)
@@ -327,6 +310,43 @@
         pltpu.VMEM((tiles * TILE, half_w), BF16),
         pltpu.VMEM((2, n_fs, tiles * TILE, fcol), F32),
     )
+    ag.drain()
+
+
+def down_kernel(
+    ep, tiles,
+    te_s, src_s, first_s, last_s, gate_s,
+    h_hbm, x_ref, w2_hbm,
+    out_ref,
+    h_ref, ring0, ring1, ring2, ring3,
+    recv_a, recv_h, recv_d,
+    in_sem, ring_sem,
+    a_send, a_recv, h_send, h_recv, d_send, d_recv,
+):
+    pc = Place(ep)
+    me, core, chips, dev = pc.me, pc.core, pc.chips, pc.dev
+    right, left, partner, far = pc.right, pc.left, pc.partner, pc.far
+    ring = (ring0, ring1, ring2, ring3)
+    tok, width = x_ref.shape
+    q_max = src_s.shape[1]
+    half_w = width // 2
+    fcol = ring0.shape[2]
+    rows_blk = tok * SUB
+
+    def tile_expert(i):
+        return te_s[0, i]
+
+    def w2_copy(cs, buf):
+        cols = pl.ds(pl.multiple_of(cs * fcol, fcol), fcol)
+        return pltpu.make_async_copy(w2_hbm.at[:, :, cols], ring[buf], ring_sem.at[buf])
+
+    h_in = pltpu.make_async_copy(h_hbm, h_ref, in_sem)
+    h_in.start()
+    for b in range(4):
+        w2_copy(b, b).start()
+    barrier = pc.signal_all()
+    pl.semaphore_wait(barrier, ep - 1)
+    h_in.wait()
 
     def phase_two(o3, pbuf, accb):
         n_slice = half_w // fcol
@@ -335,10 +355,72 @@
         p_rows = pbuf.reshape(pbuf.shape[0] // SUB, SUB, LANE)
         pbuf[q_max * SUB:(q_max + 1) * SUB, :] = jnp.zeros((SUB, LANE), F32)
 
+        def block(q, s):
+            return pl.ds(pl.multiple_of((q * ep + s) * rows_blk, rows_blk), rows_blk)
+
+        def combine(q, s):
+            un = 8
+
+            def pairs(i, run):
+                for j in range(un):
+                    qq = i * un + j
+                    row = o_rows[src_s[s, qq]]
+                    run = jnp.where(jnp.full((SUB, LANE), first_s[s, qq], jnp.int32) == 1, 0.0, run) + gate_s[s, qq] * row
+                    pbuf[pl.ds(pl.multiple_of(qq * SUB, SUB), SUB), :] = run
+                return run
+
+            lax.fori_loop(0, q_max // un, pairs, jnp.zeros((SUB, LANE), F32))
+
+            def tokens(i, carry):
+                for j in range(un):
+                    t = i * un + j
+                    dst = pl.ds(pl.multiple_of((q * ep + s) * rows_blk + t * SUB, SUB), SUB)
+                    accb[dst, :] = p_rows[last_s[s, t]]
+                return carry
+
+            lax.fori_loop(0, tok // un, tokens, 0)
+
+        def a_copy(q, j):
+            rows = pl.ds((q * chips + j) * rows_blk, rows_blk)
+            return pltpu.make_async_remote_copy(
+                accb.at[block(q, dev(order[j], 1 - core)), :], recv_a.at[rows, :], a_send.at[q, j], a_recv.at[q, j],
+                device_id={"ep": partner}, device_id_type=MESH)
+
+        def a_add(q, j):
+            a_copy(q, j).wait_recv()
+            mine = block(q, dev(order[j], core))
+            accb[mine, :] = accb[mine, :] + recv_a[(q * chips + j) * rows_blk:(q * chips + j + 1) * rows_blk, :]
+
+        hb = rows_blk // 2
+
+        def half(q, s, r):
+            return pl.ds(pl.multiple_of((q * ep + s) * rows_blk + r * hb, hb), hb)
+
+        def h_copy(q, side):
+            return pltpu.make_async_remote_copy(
+                accb.at[half(q, far, side), :], recv_h.at[pl.ds((q * 2 + side) * hb, hb), :], h_send.at[q, side], h_recv.at[q, side],
+                device_id={"ep": left if side else right}, device_id_type=MESH)
+
+        def d_copy(q, side, r):
+            s = left if side else right
+            return pltpu.make_async_remote_copy(
+                accb.at[half(q, s, r), :], recv_d.at[pl.ds((q * 2 + side) * rows_blk + r * hb, hb), :],
+                d_send.at[q, side * 2 + r], d_recv.at[q, side * 2 + r], device_id={"ep": s}, device_id_type=MESH)
+
+        def relay(q):
+            for side in range(2):
+                h_copy(q, side).wait_recv()
+                s = left if side else right
+                mine = half(q, s, side)
+                accb[mine, :] = accb[mine, :] + recv_h[(q * 2 + side) * hb:(q * 2 + side + 1) * hb, :]
+                d_copy(q, side, side).start()
+
         def down(q):
             def body(jp, carry):
                 for b1 in range(4):
                     j = jp * 4 + b1
+                    if q == 1 and b1 == 1:
+                        relay(0)
                     w2_copy(q * n_slice + j, b1).wait()
                     for i in range(tiles):
                         o = dot(h_ref[i * TILE:(i + 1) * TILE, :], ring[b1][tile_expert(i)]).astype(BF16).astype(F32)
@@ -348,67 +430,7 @@
                         w2_copy(n_slice + j, b1).start()
                 return carry
 
-            lax.fori_loop(0, n_slice // 4, body, 0)
-
-        def block(q, s):
-            return pl.ds(pl.multiple_of((q * ep + s) * rows_blk, rows_blk), rows_blk)
-
-        def combine(q, s):
-            un = 8
-
-            def pairs(i, run):
-                for j in range(un):
-                    qq = i * un + j
-                    row = o_rows[src_s[s, qq]]
-                    run = jnp.where(jnp.full((SUB, LANE), first_s[s, qq], jnp.int32) == 1, 0.0, run) + gate_s[s, qq] * row
-                    pbuf[pl.ds(pl.multiple_of(qq * SUB, SUB), SUB), :] = run
-                return run
-
-            lax.fori_loop(0, q_max // un, pairs, jnp.zeros((SUB, LANE), F32))
-
-            def tokens(i, carry):
-                for j in range(un):
-                    t = i * un + j
-                    dst = pl.ds(pl.multiple_of((q * ep + s) * rows_blk + t * SUB, SUB), SUB)
-                    accb[dst, :] = p_rows[last_s[s, t]]
-                return carry
-
-            lax.fori_loop(0, tok // un, tokens, 0)
-
-        def a_copy(q, j):
-            rows = pl.ds((q * chips + j) * rows_blk, rows_blk)
-            return pltpu.make_async_remote_copy(
-                accb.at[block(q, dev(order[j], 1 - core)), :], recv_a.at[rows, :], a_send.at[q, j], a_recv.at[q, j],
-                device_id={"ep": partner}, device_id_type=MESH)
-
-        def a_add(q, j):
-            a_copy(q, j).wait_recv()
-            mine = block(q, dev(order[j], core))
-            accb[mine, :] = accb[mine, :] + recv_a[(q * chips + j) * rows_blk:(q * chips + j + 1) * rows_blk, :]
-
-        hb = rows_blk // 2
-
-        def half(q, s, r):
-            return pl.ds(pl.multiple_of((q * ep + s) * rows_blk + r * hb, hb), hb)
-
-        def h_copy(q, side):
-            return pltpu.make_async_remote_copy(
-                accb.at[half(q, far, side), :], recv_h.at[pl.ds((q * 2 + side) * hb, hb), :], h_send.at[q, side], h_recv.at[q, side],
-                device_id={"ep": left if side else right}, device_id_type=MESH)
-
-        def d_copy(q, side, r):
-            s = left if side else right
-            return pltpu.make_async_remote_copy(
-                accb.at[half(q, s, r), :], recv_d.at[pl.ds((q * 2 + side) * rows_blk + r * hb, hb), :],
-                d_send.at[q, side * 2 + r], d_recv.at[q, side * 2 + r], device_id={"ep": s}, device_id_type=MESH)
-
-        def relay(q):
-            for side in range(2):
-                h_copy(q, side).wait_recv()
-                s = left if side else right
-                mine = half(q, s, side)
-                accb[mine, :] = accb[mine, :] + recv_h[(q * 2 + side) * hb:(q * 2 + side + 1) * hb, :]
-                d_copy(q, side, side).start()
+            body(0, 0)
 
         def scatter(q):
             for j in range(chips):
@@ -433,15 +455,13 @@
                 own = accb[pl.ds((q * ep + me) * rows_blk + v, tok, stride=SUB), :]
                 d0 = recv_d[pl.ds(q * 2 * rows_blk + v, tok, stride=SUB), :]
                 d1 = recv_d[pl.ds((q * 2 + 1) * rows_blk + v, tok, stride=SUB), :]
-                out_ref[:, cols] = (x_v[:, cols].astype(F32) + (own + d0 + d1)).astype(BF16)
+                out_ref[:, cols] = (x_ref[:, cols].astype(F32) + (own + d0 + d1)).astype(BF16)
 
         down(0)
         scatter(0)
         down(1)
-        relay(0)
         scatter(1)
         relay(1)
-        pltpu.make_async_copy(x_hbm, x_v, in_sem.at[1]).wait()
         finish(0)
         finish(1)
         for q in range(2):
@@ -458,8 +478,6 @@
         pltpu.VMEM(((q_max + 1) * SUB, LANE), F32),
         pltpu.VMEM((2 * ep * rows_blk + SUB, LANE), F32),
     )
-
-    ag.drain()
 
 
 def solution(mesh):
@@ -508,24 +526,38 @@
             ],
             compiler_params=pltpu.CompilerParams(collective_id=0, has_side_effects=True),
             name="moe_plan",
-        )(tokens, expert_ids.T, norm_gain[None, :], w_router)
-        return pl.pallas_call(
-            functools.partial(moe_kernel, ep, tiles),
-            out_shape=jax.ShapeDtypeStruct((tok, width), BF16),
-            in_specs=[sm] * 5 + [hbm, vm, vm, hbm, hbm, hbm, hbm],
+        )(tokens, expert_ids.T, norm_gain, w_router.T)
+        ring = [pltpu.VMEM((e_local, half_w, fcol), BF16)] * 4
+        h = pl.pallas_call(
+            functools.partial(up_kernel, ep, tiles),
+            out_shape=jax.ShapeDtypeStruct((tiles * TILE, ff), BF16),
+            in_specs=[sm, hbm, vm, vm, hbm, hbm],
             out_specs=vm,
             scratch_shapes=[
                 pltpu.VMEM((2, ep * tok, half_w), BF16),
-                pltpu.VMEM((tok, width), BF16),
+                *ring,
+                dma(()),
+                dma((4,)),
+                dma((14,)),
+                dma((14,)),
+            ],
+            compiler_params=pltpu.CompilerParams(
+                collective_id=1, has_side_effects=True, vmem_limit_bytes=67_043_328),
+            name="moe_up",
+        )(te, u0, u1, slot, w_gate, w_up)
+        return pl.pallas_call(
+            functools.partial(down_kernel, ep, tiles),
+            out_shape=jax.ShapeDtypeStruct((tok, width), BF16),
+            in_specs=[sm] * 5 + [hbm, vm, hbm],
+            out_specs=vm,
+            scratch_shapes=[
                 pltpu.VMEM((tiles * TILE, ff), BF16),
-                *[pltpu.VMEM((e_local, half_w, fcol), BF16)] * 4,
+                *ring,
                 pltpu.VMEM((2 * chips * rows_blk, LANE), F32),
                 pltpu.VMEM((2 * rows_blk, LANE), F32),
                 pltpu.VMEM((4 * rows_blk + SUB, LANE), F32),
-                dma((2,)),
+                dma(()),
                 dma((4,)),
-                dma((14,)),
-                dma((14,)),
                 dma((2, chips)),
                 dma((2, chips)),
                 dma((2, 2)),
@@ -534,9 +566,9 @@
                 dma((2, 4)),
             ],
             compiler_params=pltpu.CompilerParams(
-                collective_id=1, has_side_effects=True, vmem_limit_bytes=67_043_328),
-            name="moe_block",
-        )(te, src, first, last, gate, u0, u1, slot, tokens, w_gate, w_up, w_down)
+                collective_id=2, has_side_effects=True, vmem_limit_bytes=67_043_328),
+            name="moe_down",
+        )(te, src, first, last, gate, h, tokens, w_down)
 
     row_spec = P(("dp", "ep"), None)
     expert_spec = P("ep", None, None)

time: 129 us -> 132 us (1.023)
  Pallas kernels: 124 us -> 129 us
  local copies, waits for them, and re-layouts: 5.12 us -> 1.88 us
    pallas_call x1 -> x2, Pallas kernels: 100 us -> 106 us  [the longest x1 57.3 us: device_step(): pl.pallas_call(functools.partial(down_kernel, ep, tiles), out_shape=jax.S...]
    unnamed x2 -> x1, local copies, waits for them, and re-layouts: 3.83 us -> 1.88 us
where the time goes in v2:
time: 132 us; the launch traced here: 131 us
  Pallas kernels  129 us (98%)
  local copies, waits for them, and re-layouts  1.88 us (1%)
    pallas_call x1, Pallas kernels, device_step(): pl.pallas_call(functools.partial(down_kernel, ep, tiles), out_shape=jax.S...  57.3 us
    pallas_call x1, Pallas kernels, device_step(): pl.pallas_call(functools.partial(up_kernel, ep, tiles), out_shape=jax.Sha...  48.8 us
    pallas_call x1, Pallas kernels, device_step(): pl.pallas_call(functools.partial(plan_kernel, ep, tiles), out_shape=[jax....  23.3 us

profile of v2, /device:TPU:112, one launch (start us, length us, event | category | flops | bytes accessed | tf_op | source)
XLA Modules:
  0.0 131.4 jit_solution(18113254581993542972)
XLA Ops:
  0.0 23.3 %moe_plan.1 = (bf16[1024,1024]{1,0:T(8,128)(2,1)}, bf16[128,1024]{1,0:T(8,128)(2,1)}, f32[8,8,1024]{2,1,0:T(8,128)}, s32[8,256]{1,0:T(8,128)}, s32[8,256]{1,0:T(...) custom-call(bf16[128,2048]{1,0:T(8,128)(2,1)} %x_ref.3, s32[8,128]{1,0:T(8,128)} %bitcast.3, ...), custom_call_target="tpu_custom_call" | custom-call | tf_op jit(solution)/shard_map/moe_plan/pallas_call | solution.py:504
  23.4 48.8 %moe_up.1.h_hbm = bf16[2432,1024]{1,0:T(8,128)(2,1)} custom-call(s32[1,128]{1,0:T(1,128)} %get-tuple-element.13.te_s, bf16[1024,1024]{1,0:T(8,128)(2,1)} %get-tuple-element.18.u0_hbm, bf16[128,1024]{1,0:T(8,128)(2,1)} %get-tuple-element.19.u1_ref, f32[8,8,1024]{2,1,0:T(8,128)} %get-tuple-element.20.slot_ref, bf16[8,2048,1024]{2,1,0:T(8,128)(2,1)} %w1_hbm.1, ...), custom_call_target="tpu_custom_call" | custom-call | tf_op jit(solution)/shard_map/moe_up/pallas_call | solution.py:531
  72.2 57.3 %moe_down.1 = bf16[128,2048]{1,0:T(8,128)(2,1)} custom-call(s32[1,128]{1,0:T(1,128)} %get-tuple-element.13.te_s, s32[8,256]{1,0:T(8,128)} %get-tuple-element.14.src_s, s32[8,256]{1,0:T(8,128)} %get-tuple-element.15.first_s, s32[8,128]{1,0:T(8,128)} %get-tuple-element.16.last_s, f32[8,256]{1,0:T(8,128)} %get-tuple-element.17.gate_s, ...), custom_call_target="tpu_custom_call" | custom-call | tf_op jit(solution)/shard_map/moe_down/pallas_call | solution.py:548
  129.5 1.9 %copy.9 = bf16[128,2048]{1,0:T(8,128)(2,1)} copy(bf16[128,2048]{1,0:T(8,128)(2,1)} %moe_down.1) | data formatting | bytes 1048576

commit v3 on v1

--- a/solution.py
+++ b/solution.py
@@ -106,26 +106,25 @@
     pc = Place(ep)
     me = pc.me
     tok, width = x_ref.shape
-    half_w = width // 2
+    part_w = u0_ref.shape[1]
     e_local = slot_ref.shape[0]
     q_max = src_v.shape[1]
     barrier = pc.signal_all()
 
     x32 = x_ref[...].astype(F32)
     inv = lax.rsqrt(jnp.mean(x32 * x32, axis=1, keepdims=True) + NORM_EPS)
-    u_own = (x32 * inv * gain_ref[...].astype(F32)).astype(BF16)
+    u_own = (x32 * inv * gain_ref[...].astype(F32)[None, :]).astype(BF16)
     own_rows = pl.ds(pl.multiple_of(me * tok, tok), tok)
-    u0_ref[own_rows, :] = u_own[:, :half_w]
-    u1_ref[...] = u_own[:, half_w:]
+    u0_ref[own_rows, :] = u_own[:, :part_w]
+    for k in range(1, width // part_w):
+        u1_ref[k - 1] = u_own[:, k * part_w:(k + 1) * part_w]
 
     pl.semaphore_wait(barrier, ep - 1)
 
     ag = Gather(pc, u0_ref, ag_send, ag_recv, tok)
     ag.start()
 
-    logits = dot(u_own, wr_ref[...])
-    n_exp = logits.shape[1]
-    logits = jnp.concatenate([logits, jnp.zeros((tok, LANE - n_exp), F32)], axis=1).T[:n_exp]
+    logits = dot(wr_ref[...], u_own, NT_DIMS)
     ex = jnp.exp(logits - jnp.max(logits, axis=0, keepdims=True))
     p_ref[...] = ex / jnp.sum(ex, axis=0, keepdims=True)
     id_land[me] = ids_ref[...]
@@ -231,34 +230,36 @@
     tok, width = x_v.shape
     q_max = src_s.shape[1]
     half_w = width // 2
-    ff = h_ref.shape[1]
-    e_local, _, fcol = ring0.shape
-    n_fs = ff // fcol
+    part_w = ring0.shape[1]
+    parts = width // part_w
     rows_blk = tok * SUB
 
-    def w13_copy(m, buf):
-        kk, ffi = m // (2 * n_fs), (m % (2 * n_fs)) // 2
-        rows = pl.ds(pl.multiple_of(kk * half_w, half_w), half_w)
-        cols = pl.ds(pl.multiple_of(ffi * fcol, fcol), fcol)
-        return [pltpu.make_async_copy(w.at[:, rows, cols], ring[buf], ring_sem.at[buf]) for w in (w1_hbm, w3_hbm)]
-
-    def w2_copy(cs, buf):
-        cols = pl.ds(pl.multiple_of(cs * fcol, fcol), fcol)
-        return pltpu.make_async_copy(w2_hbm.at[:, :, cols], ring[buf], ring_sem.at[buf])
-
+    def up_copy(k, m):
+        w = (w1_hbm, w3_hbm)[m % 2]
+        rows = pl.ds(pl.multiple_of(k * part_w, part_w), part_w)
+        return pltpu.make_async_copy(w.at[:, rows, pl.ds(m // 2 * part_w, part_w)], ring[m], ring_sem.at[m])
+
+    def w2_copy(q, m):
+        rows = pl.ds(m % 2 * part_w, part_w)
+        return pltpu.make_async_copy(w2_hbm.at[:, rows, pl.ds((2 * q + m // 2) * part_w, part_w)], ring[m], ring_sem.at[m])
+
+    u0_in = pltpu.make_async_copy(u0_hbm, u_all.at[0], in_sem.at[0])
+    u0_in.start()
     for m in range(4):
-        w13_copy(m, m)[m % 2].start()
-
+        up_copy(0, m).start()
+    x_in = pltpu.make_async_copy(x_hbm, x_v, in_sem.at[1])
+    x_in.start()
     barrier = pc.signal_all()
-
-    pltpu.make_async_copy(u0_hbm, u_all.at[0], in_sem.at[0]).start()
-    pltpu.make_async_copy(x_hbm, x_v, in_sem.at[1]).start()
     own_rows = pl.ds(pl.multiple_of(me * tok, tok), tok)
+    for k in range(1, parts):
+        u_all[k, own_rows, :] = u1_ref[k - 1]
     pl.semaphore_wait(barrier, ep - 1)
-    ag = Gather(pc, u_all.at[1], ag_send, ag_recv, tok, own=u1_ref)
-    ag.start()
-    u_all[1, own_rows, :] = u1_ref[...]
-    pltpu.make_async_copy(u0_hbm, u_all.at[0], in_sem.at[0]).wait()
+
+    def ag(k):
+        return Gather(pc, u_all.at[k], ag_send.at[k], ag_recv.at[k], tok, own=u1_ref.at[k - 1])
+
+    ag(1).start()
+    u0_in.wait()
 
     def tile_expert(i):
         return te_s[0, i]
@@ -266,89 +267,75 @@
     def phase_one(ug, acc):
         t_iota = lax.broadcasted_iota(jnp.int32, (TILE, ep * tok), 0).astype(F32)
 
-        def gather(k, lo, hi, un):
+        def gather(k):
+            def tile(i):
+                row = slot_ref[tile_expert(i)][0:1] - lax.convert_element_type(i * TILE, F32)
+                hot = jnp.where(row == t_iota, 1.0, 0.0).astype(BF16)
+                ug[pl.ds(pl.multiple_of(i * TILE, TILE), TILE), :] = dot(hot, u_all[k]).astype(BF16)
+
+            un = 6
+            whole = tiles // un
+
             def body(g, carry):
                 for j in range(un):
-                    i = lo + g * un + j
-                    row = slot_ref[tile_expert(i)][0:1] - lax.convert_element_type(i * TILE, F32)
-                    hot = jnp.where(row == t_iota, 1.0, 0.0).astype(BF16)
-                    ug[pl.ds(pl.multiple_of(i * TILE, TILE), TILE), :] = dot(hot, u_all[k]).astype(BF16)
+                    tile(g * un + j)
                 return carry
 
-            lax.fori_loop(0, (hi - lo) // un, body, 0)
-
-        def units(k):
-            def two_units(fp, carry):
-                for b1 in (0, 2):
-                    fs = 2 * fp + b1 // 2
-                    n = k * 2 * n_fs + 2 * fs
-                    for which in range(2):
-                        w13_copy(n, b1 + which)[which].wait()
-                    for which in range(2):
-                        for i in range(tiles):
-                            rows = pl.ds(i * TILE, TILE)
-                            d = dot(ug[rows, :], ring[b1 + which][tile_expert(i)])
-                            if k == 0:
-                                acc[which, fs, rows, :] = d
-                            elif which == 0:
-                                acc[0, fs, rows, :] = acc[0, fs, rows, :] + d
-                            else:
-                                g = acc[0, fs, rows, :]
-                                hcols = pl.ds(pl.multiple_of(fs * fcol, fcol), fcol)
-                                h_ref[rows, hcols] = (g / (1.0 + jnp.exp(-g)) * (acc[1, fs, rows, :] + d)).astype(BF16)
-                        if k == 0:
-                            w13_copy(n + 4 + which, b1 + which)[which].start()
-                        else:
-                            @pl.when(fp == 0)
-                            def _():
-                                w13_copy(n + 4 + which, b1 + which)[which].start()
-
-                            @pl.when(fp > 0)
-                            def _():
-                                w2_copy(b1 + which, b1 + which).start()
-                return carry
-
-            lax.fori_loop(0, n_fs // 2, two_units, 0)
-
-        mid = tiles // 2
-        gather(0, 0, mid, 3)
-        ag.forward()
-        gather(0, mid, tiles, 5)
-        ag.rest()
-        units(0)
-        ag.last()
-        ag.finish()
-        gather(1, 0, mid, 3)
-        gather(1, mid, tiles, 5)
-        units(1)
+            lax.fori_loop(0, whole, body, 0)
+            for i in range(whole * un, tiles):
+                tile(jnp.int32(i))
+
+        def slice_dots(k, m, final):
+            fs, which = m // 2, m % 2
+            up_copy(k, m).wait()
+            for i in range(tiles):
+                rows = pl.ds(i * TILE, TILE)
+                d = dot(ug[rows, :], ring[m][tile_expert(i)])
+                if not final:
+                    acc[which, fs, rows, :] = jnp.where(k == 0, 0.0, acc[which, fs, rows, :]) + d
+                elif which == 0:
+                    acc[0, fs, rows, :] = acc[0, fs, rows, :] + d
+                else:
+                    g = acc[0, fs, rows, :]
+                    h_ref[rows, fs * part_w:(fs + 1) * part_w] = (
+                        g / (1.0 + jnp.exp(-g)) * (acc[1, fs, rows, :] + d)).astype(BF16)
+
+        def part(k, carry):
+            nxt = ag(k + 1)
+            gather(k)
+            for m in range(4):
+                slice_dots(k, m, False)
+                up_copy(k + 1, m).start()
+                if m == 0:
+                    nxt.forward()
+
+                    @pl.when(k < parts - 2)
+                    def _():
+                        ag(k + 2).start()
+                elif m == 1:
+                    nxt.rest()
+                elif m == 2:
+                    nxt.last()
+            nxt.finish()
+            return carry
+
+        lax.fori_loop(0, parts - 1, part, 0)
+        gather(parts - 1)
+        for m in range(4):
+            slice_dots(parts - 1, m, True)
+            w2_copy(0, m).start()
 
     pl.run_scoped(
         phase_one,
-        pltpu.VMEM((tiles * TILE, half_w), BF16),
-        pltpu.VMEM((2, n_fs, tiles * TILE, fcol), F32),
+        pltpu.VMEM((tiles * TILE, part_w), BF16),
+        pltpu.VMEM((2, 2, tiles * TILE, part_w), F32),
     )
 
     def phase_two(o3, pbuf, accb):
-        n_slice = half_w // fcol
         order = (2, 1, 3, 0)
         o_rows = o3.reshape(o3.shape[0] // SUB, SUB, LANE)
         p_rows = pbuf.reshape(pbuf.shape[0] // SUB, SUB, LANE)
         pbuf[q_max * SUB:(q_max + 1) * SUB, :] = jnp.zeros((SUB, LANE), F32)
-
-        def down(q):
-            def body(jp, carry):
-                for b1 in range(4):
-                    j = jp * 4 + b1
-                    w2_copy(q * n_slice + j, b1).wait()
-                    for i in range(tiles):
-                        o = dot(h_ref[i * TILE:(i + 1) * TILE, :], ring[b1][tile_expert(i)]).astype(BF16).astype(F32)
-                        for v in range(fcol // LANE):
-                            o3[pl.ds(i * TILE * SUB + j * (fcol // LANE) + v, TILE, stride=SUB), :] = o[:, v * LANE:(v + 1) * LANE]
-                    if q == 0:
-                        w2_copy(n_slice + j, b1).start()
-                return carry
-
-            lax.fori_loop(0, n_slice // 4, body, 0)
 
         def block(q, s):
             return pl.ds(pl.multiple_of((q * ep + s) * rows_blk, rows_blk), rows_blk)
@@ -409,6 +396,24 @@
                 mine = half(q, s, side)
                 accb[mine, :] = accb[mine, :] + recv_h[(q * 2 + side) * hb:(q * 2 + side + 1) * hb, :]
                 d_copy(q, side, side).start()
+
+        def down(q):
+            lanes = part_w // LANE
+            for g in range(2):
+                w2_copy(q, 2 * g).wait()
+                w2_copy(q, 2 * g + 1).wait()
+                for i in range(tiles):
+                    rows = slice(i * TILE, (i + 1) * TILE)
+                    e = tile_expert(i)
+                    o = dot(h_ref[rows, :part_w], ring[2 * g][e]) + dot(h_ref[rows, part_w:], ring[2 * g + 1][e])
+                    o = o.astype(BF16).astype(F32)
+                    for v in range(lanes):
+                        o3[pl.ds(i * TILE * SUB + g * lanes + v, TILE, stride=SUB), :] = o[:, v * LANE:(v + 1) * LANE]
+                if q == 0:
+                    w2_copy(1, 2 * g).start()
+                    w2_copy(1, 2 * g + 1).start()
+                elif g == 0:
+                    relay(0)
 
         def scatter(q):
             for j in range(chips):
@@ -438,10 +443,9 @@
         down(0)
         scatter(0)
         down(1)
-        relay(0)
         scatter(1)
         relay(1)
-        pltpu.make_async_copy(x_hbm, x_v, in_sem.at[1]).wait()
+        x_in.wait()
         finish(0)
         finish(1)
         for q in range(2):
@@ -459,7 +463,8 @@
         pltpu.VMEM((2 * ep * rows_blk + SUB, LANE), F32),
     )
 
-    ag.drain()
+    for k in range(1, parts):
+        ag(k).drain()
 
 
 def solution(mesh):
@@ -473,8 +478,7 @@
         send_max = 2 * pairs // ep
         recv_max = 3 * pairs // 2
         tiles = (recv_max + e_local * (TILE - 1)) // TILE
-        half_w = width // 2
-        fcol = 256
+        part_w = ff // 2
         chips = ep // 2
         rows_blk = tok * SUB
         vm = pl.BlockSpec(memory_space=pltpu.VMEM)
@@ -486,8 +490,8 @@
         u0, u1, slot, src, first, last, te, gate = pl.pallas_call(
             functools.partial(plan_kernel, ep, tiles),
             out_shape=[
-                jax.ShapeDtypeStruct((ep * tok, half_w), BF16),
-                jax.ShapeDtypeStruct((tok, half_w), BF16),
+                jax.ShapeDtypeStruct((ep * tok, part_w), BF16),
+                jax.ShapeDtypeStruct((width // part_w - 1, tok, part_w), BF16),
                 jax.ShapeDtypeStruct((e_local, SUB, ep * tok), F32),
                 jax.ShapeDtypeStruct(groups, i32),
                 jax.ShapeDtypeStruct(groups, i32),
@@ -508,24 +512,24 @@
             ],
             compiler_params=pltpu.CompilerParams(collective_id=0, has_side_effects=True),
             name="moe_plan",
-        )(tokens, expert_ids.T, norm_gain[None, :], w_router)
+        )(tokens, expert_ids.T, norm_gain, w_router.T)
         return pl.pallas_call(
             functools.partial(moe_kernel, ep, tiles),
             out_shape=jax.ShapeDtypeStruct((tok, width), BF16),
             in_specs=[sm] * 5 + [hbm, vm, vm, hbm, hbm, hbm, hbm],
             out_specs=vm,
             scratch_shapes=[
-                pltpu.VMEM((2, ep * tok, half_w), BF16),
+                pltpu.VMEM((width // part_w, ep * tok, part_w), BF16),
                 pltpu.VMEM((tok, width), BF16),
                 pltpu.VMEM((tiles * TILE, ff), BF16),
-                *[pltpu.VMEM((e_local, half_w, fcol), BF16)] * 4,
+                *[pltpu.VMEM((e_local, part_w, part_w), BF16)] * 4,
                 pltpu.VMEM((2 * chips * rows_blk, LANE), F32),
                 pltpu.VMEM((2 * rows_blk, LANE), F32),
                 pltpu.VMEM((4 * rows_blk + SUB, LANE), F32),
                 dma((2,)),
                 dma((4,)),
-                dma((14,)),
-                dma((14,)),
+                dma((width // part_w, 14)),
+                dma((width // part_w, 14)),
                 dma((2, chips)),
                 dma((2, chips)),
                 dma((2, 2)),

time: 129 us -> 116 us (0.90)
  Pallas kernels: 124 us -> 114 us
  local copies, waits for them, and re-layouts: 5.12 us -> 1.88 us
    pallas_call x1, Pallas kernels: 100 us -> 95.1 us  [device_step(): pl.pallas_call(functools.partial(moe_kernel, ep, tiles), out_shape=jax.Sh...]
    pallas_call x1, Pallas kernels: 23.4 us -> 18.7 us  [device_step(): pl.pallas_call(functools.partial(plan_kernel, ep, tiles), out_shape=[jax....]
    unnamed x2 -> x1, local copies, waits for them, and re-layouts: 3.83 us -> 1.88 us
where the time goes in v3:
time: 116 us
  Pallas kernels  114 us (98%)
  local copies, waits for them, and re-layouts  1.88 us (2%)
    pallas_call x1, Pallas kernels, device_step(): pl.pallas_call(functools.partial(moe_kernel, ep, tiles), out_shape=jax.Sh...  95.1 us
    pallas_call x1, Pallas kernels, device_step(): pl.pallas_call(functools.partial(plan_kernel, ep, tiles), out_shape=[jax....  18.7 us

profile of v3, /device:TPU:112, one launch (start us, length us, event | category | flops | bytes accessed | tf_op | source)
XLA Modules:
  0.0 115.7 jit_solution(14652279939049162578)
XLA Ops:
  0.0 18.7 %moe_plan.1 = (bf16[1024,512]{1,0:T(8,128)(2,1)}, bf16[3,128,512]{2,1,0:T(8,128)(2,1)}, f32[8,8,1024]{2,1,0:T(8,128)}, s32[8,256]{1,0:T(8,128)}, s32[8,256]{1,0:...) custom-call(bf16[128,2048]{1,0:T(8,128)(2,1)} %x_hbm.1, s32[8,128]{1,0:T(8,128)} %bitcast.3, ...), custom_call_target="tpu_custom_call" | custom-call | tf_op jit(solution)/shard_map/moe_plan/pallas_call | solution.py:490
  18.7 95.1 %moe_block.1 = bf16[128,2048]{1,0:T(8,128)(2,1)} custom-call(s32[1,128]{1,0:T(1,128)} %get-tuple-element.13.te_s, s32[8,256]{1,0:T(8,128)} %get-tuple-element.14.src_s, s32[8,256]{1,0:T(8,128)} %get-tuple-element.15.first_s, s32[8,128]{1,0:T(8,128)} %get-tuple-element.16.last_s, f32[8,256]{1,0:T(8,128)} %get-tuple-element.17.gate_s, ...), custom_call_target="tpu_custom_call" | custom-call | tf_op jit(solution)/shard_map/moe_block/pallas_call | solution.py:516
  113.8 1.9 %copy.9 = bf16[128,2048]{1,0:T(8,128)(2,1)} copy(bf16[128,2048]{1,0:T(8,128)(2,1)} %moe_block.1) | data formatting | bytes 1048576

commit v4 on v3

--- a/solution.py
+++ b/solution.py
@@ -98,18 +98,24 @@
 
 def plan_kernel(
     ep, tiles,
-    x_ref, ids_ref, gain_ref, wr_ref,
+    x_hbm, ids_hbm, gain_hbm, wr_hbm,
     u0_ref, u1_ref, slot_ref, src_v, first_v, last_v, te_v, gate_v,
-    p_ref, id_land, p_land,
-    small_send, small_recv, ag_send, ag_recv,
+    x_ref, ids_ref, gain_ref, wr_ref, p_ref, id_land, p_land,
+    in_sem, small_send, small_recv, ag_send, ag_recv,
 ):
     pc = Place(ep)
     me = pc.me
+    ops_in = [pltpu.make_async_copy(a, b, in_sem.at[i]) for i, (a, b) in enumerate(
+        ((x_hbm, x_ref), (gain_hbm, gain_ref), (wr_hbm, wr_ref), (ids_hbm, ids_ref)))]
+    for c in ops_in:
+        c.start()
     tok, width = x_ref.shape
     part_w = u0_ref.shape[1]
     e_local = slot_ref.shape[0]
-    q_max = src_v.shape[1]
+    q_max = src_v.shape[0] * LANE // ep
     barrier = pc.signal_all()
+    for c in ops_in:
+        c.wait()
 
     x32 = x_ref[...].astype(F32)
     inv = lax.rsqrt(jnp.mean(x32 * x32, axis=1, keepdims=True) + NORM_EPS)
@@ -199,9 +205,13 @@
         sel = got[0:e8] == q_lane
         src = jnp.sum(jnp.where(sel, got[e8:2 * e8] * 64.0 + got[2 * e8:3 * e8], 0.0), axis=0, keepdims=True)
         gate = jnp.sum(jnp.where(sel, got[4 * e8:5 * e8] + got[5 * e8:6 * e8] + got[6 * e8:7 * e8], 0.0), axis=0, keepdims=True)
-        src_v[b:b + 1, :] = jnp.clip(src.astype(jnp.int32), 0, tiles * TILE - 1)
-        first_v[b:b + 1, :] = (got[3 * e8:3 * e8 + 1] == q_lane[0:1]).astype(jnp.int32)
-        gate_v[b:b + 1, :] = gate
+        src = jnp.clip(src.astype(jnp.int32), 0, tiles * TILE - 1)
+        first = (got[3 * e8:3 * e8 + 1] == q_lane[0:1]).astype(jnp.int32)
+        for v in range(q_max // LANE):
+            r, lanes = b * (q_max // LANE) + v, slice(v * LANE, (v + 1) * LANE)
+            src_v[r:r + 1, :] = src[:, lanes]
+            first_v[r:r + 1, :] = first[:, lanes]
+            gate_v[r:r + 1, :] = gate[:, lanes]
 
     ag.forward()
     ag.rest()
@@ -215,9 +225,10 @@
 
 def moe_kernel(
     ep, tiles,
-    te_s, src_s, first_s, last_s, gate_s,
-    u0_hbm, u1_ref, slot_ref, x_hbm, w1_hbm, w3_hbm, w2_hbm,
+    te_hbm, src_hbm, first_hbm, last_hbm, gate_hbm,
+    u0_hbm, u1_hbm, slot_hbm, x_hbm, w1_hbm, w3_hbm, w2_hbm,
     out_ref,
+    te_s, src_s, first_s, last_s, gate_s, u1_ref, slot_ref,
     u_all, x_v, h_ref, ring0, ring1, ring2, ring3,
     recv_a, recv_h, recv_d,
     in_sem, ring_sem, ag_send, ag_recv,
@@ -228,7 +239,7 @@
     right, left, partner, far = pc.right, pc.left, pc.partner, pc.far
     ring = (ring0, ring1, ring2, ring3)
     tok, width = x_v.shape
-    q_max = src_s.shape[1]
+    q_max = src_s.shape[0] // ep
     half_w = width // 2
     part_w = ring0.shape[1]
     parts = width // part_w
@@ -243,14 +254,18 @@
         rows = pl.ds(m % 2 * part_w, part_w)
         return pltpu.make_async_copy(w2_hbm.at[:, rows, pl.ds((2 * q + m // 2) * part_w, part_w)], ring[m], ring_sem.at[m])
 
-    u0_in = pltpu.make_async_copy(u0_hbm, u_all.at[0], in_sem.at[0])
-    u0_in.start()
+    barrier = pc.signal_all()
+    pairs_in = ((u1_hbm, u1_ref), (u0_hbm, u_all.at[0]), (te_hbm, te_s), (slot_hbm, slot_ref), (src_hbm, src_s),
+                (first_hbm, first_s), (last_hbm, last_s), (gate_hbm, gate_s), (x_hbm, x_v))
+    ops_in = [pltpu.make_async_copy(a, b, in_sem.at[i]) for i, (a, b) in enumerate(pairs_in)]
+    for c in ops_in[:4]:
+        c.start()
     for m in range(4):
         up_copy(0, m).start()
-    x_in = pltpu.make_async_copy(x_hbm, x_v, in_sem.at[1])
-    x_in.start()
-    barrier = pc.signal_all()
+    for c in ops_in[4:]:
+        c.start()
     own_rows = pl.ds(pl.multiple_of(me * tok, tok), tok)
+    ops_in[0].wait()
     for k in range(1, parts):
         u_all[k, own_rows, :] = u1_ref[k - 1]
     pl.semaphore_wait(barrier, ep - 1)
@@ -259,7 +274,8 @@
         return Gather(pc, u_all.at[k], ag_send.at[k], ag_recv.at[k], tok, own=u1_ref.at[k - 1])
 
     ag(1).start()
-    u0_in.wait()
+    for c in ops_in[1:4]:
+        c.wait()
 
     def tile_expert(i):
         return te_s[0, i]
@@ -303,19 +319,26 @@
         def part(k, carry):
             nxt = ag(k + 1)
             gather(k)
+
+            def pass_on():
+                nxt.forward()
+
+                @pl.when(k < parts - 2)
+                def _():
+                    ag(k + 2).start()
+
+            pl.when(k > 0)(pass_on)
             for m in range(4):
                 slice_dots(k, m, False)
                 up_copy(k + 1, m).start()
                 if m == 0:
-                    nxt.forward()
-
-                    @pl.when(k < parts - 2)
-                    def _():
-                        ag(k + 2).start()
+                    pl.when(k == 0)(pass_on)
                 elif m == 1:
                     nxt.rest()
                 elif m == 2:
-                    nxt.last()
+                    pl.when(k > 0)(nxt.last)
+                else:
+                    pl.when(k == 0)(nxt.last)
             nxt.finish()
             return carry
 
@@ -341,23 +364,24 @@
             return pl.ds(pl.multiple_of((q * ep + s) * rows_blk, rows_blk), rows_blk)
 
         def combine(q, s):
-            un = 8
+            un = 16
 
             def pairs(i, run):
+                at = s * q_max + i * un
                 for j in range(un):
-                    qq = i * un + j
-                    row = o_rows[src_s[s, qq]]
-                    run = jnp.where(jnp.full((SUB, LANE), first_s[s, qq], jnp.int32) == 1, 0.0, run) + gate_s[s, qq] * row
-                    pbuf[pl.ds(pl.multiple_of(qq * SUB, SUB), SUB), :] = run
+                    row = o_rows[src_s[at + j]]
+                    is_first = jnp.full((SUB, LANE), first_s[at + j], jnp.int32) == 1
+                    run = jnp.where(is_first, 0.0, run) + gate_s[at + j] * row
+                    pbuf[pl.ds(pl.multiple_of((i * un + j) * SUB, SUB), SUB), :] = run
                 return run
 
             lax.fori_loop(0, q_max // un, pairs, jnp.zeros((SUB, LANE), F32))
 
             def tokens(i, carry):
+                at = s * tok + i * un
                 for j in range(un):
-                    t = i * un + j
-                    dst = pl.ds(pl.multiple_of((q * ep + s) * rows_blk + t * SUB, SUB), SUB)
-                    accb[dst, :] = p_rows[last_s[s, t]]
+                    dst = pl.ds(pl.multiple_of((q * ep + s) * rows_blk + (i * un + j) * SUB, SUB), SUB)
+                    accb[dst, :] = p_rows[last_s[at + j]]
                 return carry
 
             lax.fori_loop(0, tok // un, tokens, 0)
@@ -416,10 +440,7 @@
                     relay(0)
 
         def scatter(q):
-            for j in range(chips):
-                combine(q, dev(order[j], 1 - core))
-                a_copy(q, j).start()
-                combine(q, dev(order[j], core))
+            def settle(j):
                 a_add(q, j)
                 if j == 0:
                     h_copy(q, 0).start()
@@ -428,6 +449,14 @@
                     d_copy(q, 0, 1).start()
                 elif j == 2:
                     d_copy(q, 1, 0).start()
+
+            for j in range(chips):
+                combine(q, dev(order[j], 1 - core))
+                a_copy(q, j).start()
+                combine(q, dev(order[j], core))
+                if j > 0:
+                    settle(j - 1)
+            settle(chips - 1)
 
         def finish(q):
             for side in range(2):
@@ -441,11 +470,13 @@
                 out_ref[:, cols] = (x_v[:, cols].astype(F32) + (own + d0 + d1)).astype(BF16)
 
         down(0)
+        for c in ops_in[4:8]:
+            c.wait()
         scatter(0)
         down(1)
         scatter(1)
         relay(1)
-        x_in.wait()
+        ops_in[8].wait()
         finish(0)
         finish(1)
         for q in range(2):
@@ -483,10 +514,9 @@
         rows_blk = tok * SUB
         vm = pl.BlockSpec(memory_space=pltpu.VMEM)
         hbm = pl.BlockSpec(memory_space=pl.ANY)
-        sm = pl.BlockSpec(memory_space=pltpu.SMEM)
         dma = pltpu.SemaphoreType.DMA
         i32 = jnp.int32
-        groups = (ep, send_max)
+        groups = (ep * send_max // LANE, LANE)
         u0, u1, slot, src, first, last, te, gate = pl.pallas_call(
             functools.partial(plan_kernel, ep, tiles),
             out_shape=[
@@ -499,12 +529,17 @@
                 jax.ShapeDtypeStruct((1, LANE), i32),
                 jax.ShapeDtypeStruct(groups, F32),
             ],
-            in_specs=[vm] * 4,
+            in_specs=[hbm] * 4,
             out_specs=[vm] * 8,
             scratch_shapes=[
+                pltpu.VMEM((tok, width), BF16),
+                pltpu.VMEM((top_k, tok), i32),
+                pltpu.VMEM((width,), BF16),
+                pltpu.VMEM((w_router.shape[1], width), BF16),
                 pltpu.VMEM((w_router.shape[1], tok), F32),
                 pltpu.VMEM((ep, top_k, tok), i32),
                 pltpu.VMEM((ep, e_local, tok), F32),
+                dma((4,)),
                 dma((2, ep)),
                 dma((2, ep)),
                 dma((14,)),
@@ -516,9 +551,16 @@
         return pl.pallas_call(
             functools.partial(moe_kernel, ep, tiles),
             out_shape=jax.ShapeDtypeStruct((tok, width), BF16),
-            in_specs=[sm] * 5 + [hbm, vm, vm, hbm, hbm, hbm, hbm],
+            in_specs=[hbm] * 12,
             out_specs=vm,
             scratch_shapes=[
+                pltpu.SMEM((1, LANE), i32),
+                pltpu.SMEM((ep * send_max,), i32),
+                pltpu.SMEM((ep * send_max,), i32),
+                pltpu.SMEM((ep * tok,), i32),
+                pltpu.SMEM((ep * send_max,), F32),
+                pltpu.VMEM((width // part_w - 1, tok, part_w), BF16),
+                pltpu.VMEM((e_local, SUB, ep * tok), F32),
                 pltpu.VMEM((width // part_w, ep * tok, part_w), BF16),
                 pltpu.VMEM((tok, width), BF16),
                 pltpu.VMEM((tiles * TILE, ff), BF16),
@@ -526,7 +568,7 @@
                 pltpu.VMEM((2 * chips * rows_blk, LANE), F32),
                 pltpu.VMEM((2 * rows_blk, LANE), F32),
                 pltpu.VMEM((4 * rows_blk + SUB, LANE), F32),
-                dma((2,)),
+                dma((9,)),
                 dma((4,)),
                 dma((width // part_w, 14)),
                 dma((width // part_w, 14)),
@@ -540,7 +582,7 @@
             compiler_params=pltpu.CompilerParams(
                 collective_id=1, has_side_effects=True, vmem_limit_bytes=67_043_328),
             name="moe_block",
-        )(te, src, first, last, gate, u0, u1, slot, tokens, w_gate, w_up, w_down)
+        )(te, src.reshape(-1), first.reshape(-1), last.reshape(-1), gate.reshape(-1), u0, u1, slot, tokens, w_gate, w_up, w_down)
 
     row_spec = P(("dp", "ep"), None)
     expert_spec = P("ep", None, None)

time: 116 us -> 109 us (0.940)
  Pallas kernels: 114 us -> 107 us
    pallas_call x1, Pallas kernels: 95.1 us -> 89.6 us  [device_step(): pl.pallas_call(functools.partial(moe_kernel, ep, tiles), out_shape=jax.Sh...]
where the time goes in v4:
time: 109 us
  Pallas kernels  107 us (98%)
  local copies, waits for them, and re-layouts  1.88 us (2%)
    pallas_call x1, Pallas kernels, device_step(): pl.pallas_call(functools.partial(moe_kernel, ep, tiles), out_shape=jax.Sh...  89.6 us
    pallas_call x1, Pallas kernels, device_step(): pl.pallas_call(functools.partial(plan_kernel, ep, tiles), out_shape=[jax....  17.7 us

profile of v4, /device:TPU:112, one launch (start us, length us, event | category | flops | bytes accessed | tf_op | source)
XLA Modules:
  0.0 109.2 jit_solution(2512995702793005284)
XLA Ops:
  0.0 17.7 %moe_plan.1 = (bf16[1024,512]{1,0:T(8,128)(2,1)}, bf16[3,128,512]{2,1,0:T(8,128)(2,1)}, f32[8,8,1024]{2,1,0:T(8,128)}, s32[16,128]{1,0:T(8,128)}, s32[16,128]{1,...) custom-call(bf16[128,2048]{1,0:T(8,128)(2,1)} %x_hbm.3, s32[8,128]{1,0:T(8,128)} %bitcast.10, ...), custom_call_target="tpu_custom_call" | custom-call | tf_op jit(solution)/shard_map/moe_plan/pallas_call | solution.py:520
  17.7 89.6 %moe_block.1 = bf16[128,2048]{1,0:T(8,128)(2,1)} custom-call(s32[1,128]{1,0:T(1,128)} %get-tuple-element.13.te_hbm, s32[2048]{0:T(1024)} %bitcast.7, s32[2048]{0:T(1024)} %bitcast.8, s32[1024]{0:T(1024)} %bitcast.11, f32[2048]{0:T(1024)} %bitcast.9, bf16[1024,512]{1,0:T(8,128)(2,1)} %get-tuple-element.18.u0_hbm, ...), custom_call_target="tpu_custom_call" | custom-call | tf_op jit(solution)/shard_map/moe_block/pallas_call | solution.py:551
  107.3 1.9 %copy.9 = bf16[128,2048]{1,0:T(8,128)(2,1)} copy(bf16[128,2048]{1,0:T(8,128)(2,1)} %moe_block.1) | data formatting | bytes 1048576

commit v5 on v4

--- a/solution.py
+++ b/solution.py
@@ -285,25 +285,17 @@
 
         def gather(k):
             def tile(i):
-                row = slot_ref[tile_expert(i)][0:1] - lax.convert_element_type(i * TILE, F32)
+                row = slot_ref[tile_expert(i)][0:1] - float(i * TILE)
                 hot = jnp.where(row == t_iota, 1.0, 0.0).astype(BF16)
-                ug[pl.ds(pl.multiple_of(i * TILE, TILE), TILE), :] = dot(hot, u_all[k]).astype(BF16)
-
-            un = 6
-            whole = tiles // un
-
-            def body(g, carry):
-                for j in range(un):
-                    tile(g * un + j)
-                return carry
-
-            lax.fori_loop(0, whole, body, 0)
-            for i in range(whole * un, tiles):
-                tile(jnp.int32(i))
+                ug[i * TILE:(i + 1) * TILE, :] = dot(hot, u_all[k]).astype(BF16)
+
+            for i in range(tiles):
+                tile(i)
 
         def slice_dots(k, m, final):
             fs, which = m // 2, m % 2
-            up_copy(k, m).wait()
+            if not final:
+                up_copy(k, m).wait()
             for i in range(tiles):
                 rows = pl.ds(i * TILE, TILE)
                 d = dot(ug[rows, :], ring[m][tile_expert(i)])
@@ -344,6 +336,8 @@
 
         lax.fori_loop(0, parts - 1, part, 0)
         gather(parts - 1)
+        for m in range(4):
+            up_copy(parts - 1, m).wait()
         for m in range(4):
             slice_dots(parts - 1, m, True)
             w2_copy(0, m).start()
@@ -436,8 +430,6 @@
                 if q == 0:
                     w2_copy(1, 2 * g).start()
                     w2_copy(1, 2 * g + 1).start()
-                elif g == 0:
-                    relay(0)
 
         def scatter(q):
             def settle(j):
@@ -474,10 +466,11 @@
             c.wait()
         scatter(0)
         down(1)
+        relay(0)
         scatter(1)
-        relay(1)
         ops_in[8].wait()
         finish(0)
+        relay(1)
         finish(1)
         for q in range(2):
             for j in range(chips):

time: 109 us -> 107 us (0.982)
  Pallas kernels: 107 us -> 105 us
    pallas_call x1, Pallas kernels: 89.6 us -> 87.6 us  [device_step(): pl.pallas_call(functools.partial(moe_kernel, ep, tiles), out_shape=jax.Sh...]
where the time goes in v5:
time: 107 us
  Pallas kernels  105 us (98%)
  local copies, waits for them, and re-layouts  1.88 us (2%)
    pallas_call x1, Pallas kernels, device_step(): pl.pallas_call(functools.partial(moe_kernel, ep, tiles), out_shape=jax.Sh...  87.6 us
    pallas_call x1, Pallas kernels, device_step(): pl.pallas_call(functools.partial(plan_kernel, ep, tiles), out_shape=[jax....  17.7 us

profile of v5, /device:TPU:112, one launch (start us, length us, event | category | flops | bytes accessed | tf_op | source)
XLA Modules:
  0.0 107.1 jit_solution(9035921976330980119)
XLA Ops:
  0.0 17.7 %moe_plan.1 = (bf16[1024,512]{1,0:T(8,128)(2,1)}, bf16[3,128,512]{2,1,0:T(8,128)(2,1)}, f32[8,8,1024]{2,1,0:T(8,128)}, s32[16,128]{1,0:T(8,128)}, s32[16,128]{1,...) custom-call(bf16[128,2048]{1,0:T(8,128)(2,1)} %x_hbm.3, s32[8,128]{1,0:T(8,128)} %bitcast.10, ...), custom_call_target="tpu_custom_call" | custom-call | tf_op jit(solution)/shard_map/moe_plan/pallas_call | solution.py:513
  17.7 87.6 %moe_block.1 = bf16[128,2048]{1,0:T(8,128)(2,1)} custom-call(s32[1,128]{1,0:T(1,128)} %get-tuple-element.13.te_hbm, s32[2048]{0:T(1024)} %bitcast.7, s32[2048]{0:T(1024)} %bitcast.8, s32[1024]{0:T(1024)} %bitcast.11, f32[2048]{0:T(1024)} %bitcast.9, bf16[1024,512]{1,0:T(8,128)(2,1)} %get-tuple-element.18.u0_hbm, ...), custom_call_target="tpu_custom_call" | custom-call | tf_op jit(solution)/shard_map/moe_block/pallas_call | solution.py:544
  105.3 1.9 %copy.9 = bf16[128,2048]{1,0:T(8,128)(2,1)} copy(bf16[128,2048]{1,0:T(8,128)(2,1)} %moe_block.1) | data formatting | bytes 1048576
